TPU v7x, 32 devices: a whole 2x2x4 slice. The times are simulated.
32 devices in a mesh: dpy: 4 (over z), dpx: 2 (over y), tp: 4 (over x, core).
Axes of the slice: x: 2, y: 2, z: 4, core: 2. Of those that a mesh axis runs over, the one named last changes fastest.
Arguments:
- x_saved: bfloat16 [2, 16, 1024, 1536], P(None, ('dpy', 'dpx'))
- y_saved: bfloat16 [2, 16, 1024, 1536], P(None, ('dpy', 'dpx'))
- d_out: bfloat16 [16, 1024, 1536], P(('dpy', 'dpx'))
- w_qkv: bfloat16 [2, 1536, 3, 12, 128], P(None, None, None, 'tp')
- w_out: bfloat16 [2, 12, 128, 1536], P(None, 'tp')
- w_up: bfloat16 [2, 1536, 6144], P(None, None, 'tp')
- w_down: bfloat16 [2, 6144, 1536], P(None, 'tp')
Outputs:
- output 1: bfloat16 [16, 1024, 1536], P(('dpy', 'dpx'))
- output 2: float32 [2, 1536, 3, 12, 128], P(None, None, None, 'tp')
- output 3: float32 [2, 12, 128, 1536], P(None, 'tp')
- output 4: float32 [2, 1536, 6144], P(None, None, 'tp')
- output 5: float32 [2, 6144, 1536], P(None, 'tp')
All inputs are finite; a program needn't handle non-finite values.
Results may differ from a plain program's by a relative error of at most 0.02.
Values are sent between devices in bfloat16 or wider.
A program may use at most 1 GiB of HBM per device.

v0:
```python
import jax
import jax.numpy as jnp
from jax import lax
from jax.sharding import PartitionSpec as P

MICROBATCHES = 2


def layer_backward(x_in, y_mid, grad_out, wqkv_l, wout_l, wup_l, wdown_l):
    hidden = jnp.einsum('bsh,hf->bsf', y_mid, wup_l, preferred_element_type=jnp.float32)
    act_f32, gelu_pull = jax.vjp(jax.nn.gelu, hidden)
    act_b = act_f32.astype(jnp.bfloat16)
    g_down = jnp.einsum('bsf,bsh->fh', act_b, grad_out, preferred_element_type=jnp.float32)
    d_act = jnp.einsum('bsh,fh->bsf', grad_out, wdown_l, preferred_element_type=jnp.float32)
    d_hidden = gelu_pull(d_act)[0].astype(jnp.bfloat16)
    g_up = jnp.einsum('bsh,bsf->hf', y_mid, d_hidden, preferred_element_type=jnp.float32)
    mid_part = jnp.einsum('bsf,hf->bsh', d_hidden, wup_l, preferred_element_type=jnp.float32).astype(jnp.bfloat16)
    mid_sum = lax.psum(mid_part, 'tp')
    d_mid = (grad_out.astype(jnp.float32) + mid_sum.astype(jnp.float32)).astype(jnp.bfloat16)
    scale_factor = wqkv_l.shape[-1] ** -0.5
    queries = jnp.einsum('bsh,hnd->bsnd', x_in, wqkv_l[:, 0], preferred_element_type=jnp.float32).astype(jnp.bfloat16)
    keys_all = jnp.einsum('bsh,hnd->bsnd', x_in, wqkv_l[:, 1], preferred_element_type=jnp.float32).astype(jnp.bfloat16)
    values = jnp.einsum('bsh,hnd->bsnd', x_in, wqkv_l[:, 2], preferred_element_type=jnp.float32).astype(jnp.bfloat16)
    scores = jnp.einsum('bqnd,bknd->bnqk', queries, keys_all, preferred_element_type=jnp.float32) * scale_factor
    probs_f = jax.nn.softmax(scores, axis=-1)
    probs_b = probs_f.astype(jnp.bfloat16)
    att_out = jnp.einsum('bnqk,bknd->bqnd', probs_b, values, preferred_element_type=jnp.float32).astype(jnp.bfloat16)
    d_att = jnp.einsum('bsh,ndh->bsnd', d_mid, wout_l, preferred_element_type=jnp.float32).astype(jnp.bfloat16)
    g_out = jnp.einsum('bsnd,bsh->ndh', att_out, d_mid, preferred_element_type=jnp.float32)
    d_probs = jnp.einsum('bqnd,bknd->bnqk', d_att, values, preferred_element_type=jnp.float32)
    d_values = jnp.einsum('bnqk,bqnd->bknd', probs_b, d_att, preferred_element_type=jnp.float32).astype(jnp.bfloat16)
    row_dot = jnp.sum(d_probs * probs_f, axis=-1, keepdims=True)
    d_scores = (probs_f * (d_probs - row_dot) * scale_factor).astype(jnp.bfloat16)
    d_queries = jnp.einsum('bnqk,bknd->bqnd', d_scores, keys_all, preferred_element_type=jnp.float32).astype(jnp.bfloat16)
    d_keys = jnp.einsum('bnqk,bqnd->bknd', d_scores, queries, preferred_element_type=jnp.float32).astype(jnp.bfloat16)
    d_qkv = jnp.stack([d_queries, d_keys, d_values], axis=2)
    g_qkv = jnp.einsum('bsh,bscnd->hcnd', x_in, d_qkv, preferred_element_type=jnp.float32)
    in_part = jnp.einsum('bscnd,hcnd->bsh', d_qkv, wqkv_l, preferred_element_type=jnp.float32).astype(jnp.bfloat16)
    in_sum = lax.psum(in_part, 'tp')
    d_in = (d_mid.astype(jnp.float32) + in_sum.astype(jnp.float32)).astype(jnp.bfloat16)
    return d_in, (g_qkv, g_out, g_up, g_down)


def solution(mesh):
    data_axes = ('dpy', 'dpx')
    replicas = mesh.shape['dpy'] * mesh.shape['dpx']
    act_spec = P(None, data_axes, None, None)
    tok_spec = P(data_axes, None, None)
    qkv_spec = P(None, None, None, 'tp', None)
    wout_spec = P(None, 'tp', None, None)
    up_spec = P(None, None, 'tp')
    down_spec = P(None, 'tp', None)

    def device_backward(x_saved, y_saved, d_out, w_qkv, w_out, w_up, w_down):
        num_layers = w_qkv.shape[0]
        micro_rows = d_out.shape[0] // MICROBATCHES
        grad_acc = [None] * num_layers
        d_inputs = []
        for micro_idx in range(MICROBATCHES):
            row_range = slice(micro_idx * micro_rows, (micro_idx + 1) * micro_rows)
            grad_cur = d_out[row_range]
            for layer_idx in reversed(range(num_layers)):
                grad_cur, grads_new = layer_backward(x_saved[layer_idx, row_range], y_saved[layer_idx, row_range], grad_cur, w_qkv[layer_idx], w_out[layer_idx], w_up[layer_idx], w_down[layer_idx])
                if micro_idx == 0:
                    grad_acc[layer_idx] = grads_new
                else:
                    grad_acc[layer_idx] = tuple(grad_prev + grad_next for grad_prev, grad_next in zip(grad_acc[layer_idx], grads_new))
                if micro_idx == MICROBATCHES - 1:
                    grad_acc[layer_idx] = tuple(lax.psum(grad_sum, data_axes) / replicas for grad_sum in grad_acc[layer_idx])
            d_inputs.append(grad_cur)
        stacked = tuple(jnp.stack([grad_set[slot_idx] for grad_set in grad_acc]) for slot_idx in range(4))
        return (jnp.concatenate(d_inputs, axis=0),) + stacked

    return jax.shard_map(device_backward, mesh=mesh, in_specs=(act_spec, act_spec, tok_spec, qkv_spec, wout_spec, up_spec, down_spec), out_specs=(tok_spec, qkv_spec, wout_spec, up_spec, down_spec), check_vma=False)
```

profile of v0, /device:TPU:0, one launch (start us, length us, event | category | flops | bytes accessed | tf_op | source)
XLA Modules:
  0.0 2668.9 jit_solution(16741673799598886487)
XLA Ops:
  7.3 9.8 fusion.110
  17.1 9.7 fusion.106
  26.8 10.0 fusion.38
  38.5 6.5 fusion.153
  45.0 10.0 fusion.52
  56.7 6.4 fusion.150
  63.4 9.8 fusion.94
  73.3 11.1 fusion.161
  84.4 6.9 fusion.90
  91.3 8.1 fusion.221
  135.6 9.7 add_bitcast_fusion
  145.4 10.1 fusion.505
  155.4 10.7 fusion.504
  166.1 10.5 fusion.507
  176.6 4.8 fusion.354
  181.4 10.5 fusion.506
  191.9 12.4 convolution_add_fusion
  204.3 7.1 add_convert_fusion.7
  213.3 6.6 fusion.508
  223.1 19.5 fusion.420
  242.6 19.0 fusion.423
  265.9 6.7 fusion.510
  275.8 19.5 fusion.432
  295.3 19.3 fusion.435
  314.6 9.6 fusion.182
  324.2 8.8 fusion.156
  333.0 7.7 fusion.158
  340.8 6.6 fusion.163
  347.4 8.1 add_bitcast_fusion.2
  355.5 9.3 fusion.266
  364.8 98.2 %all-reduce.17.cloned.1.call-done = (bf16[1,1024,1536]{2,1,0:T(8,128)(2,1)}, bf16[1,1024,1536]{2,1,0:T(8,128)(2,1)}) async-done(((bf16[1,1024,1536]{2,1,0:T(8,128)(2,1)}, bf16[1,1024,1536]{2,1,0:T(8,128)(2,1)}), (bf16[1,1024,1536]{2,1,0:T(8,128)(2,1)}, bf16[1,1024,1536]{2,1,0:T(8,128)(2,1)})) %all-reduce.17.cloned.1.call-update) | async-done | bytes 6291472 | tf_op jit(solution)/shard_map/psum | solution.py:39
  463.0 13.3 fusion.45
  476.3 11.5 fusion.160
  487.9 9.0 fusion.147
  496.9 10.2 fusion.206
  507.2 9.6 fusion.59
  516.7 9.3 fusion.144
  526.1 11.7 add_bitcast_fusion.1
  537.8 13.0 convolution_add_fusion.1
  550.8 95.0 %all-reduce.15.cloned.1.call-done = (bf16[1,1024,1536]{2,1,0:T(8,128)(2,1)}, bf16[1,1024,1536]{2,1,0:T(8,128)(2,1)}) async-done(((bf16[1,1024,1536]{2,1,0:T(8,128)(2,1)}, bf16[1,1024,1536]{2,1,0:T(8,128)(2,1)}), (bf16[1,1024,1536]{2,1,0:T(8,128)(2,1)}, bf16[1,1024,1536]{2,1,0:T(8,128)(2,1)})) %all-reduce.15.cloned.1.call-update) | async-done | bytes 6291472 | tf_op jit(solution)/shard_map/psum | solution.py:18
  645.8 8.3 add_convert_fusion.1
  656.0 7.6 fusion.509
  666.7 19.0 fusion.426
  685.7 19.4 fusion.429
  708.5 6.7 fusion.511
  718.4 19.5 fusion.438
  737.8 19.2 fusion.441
  757.0 8.6 fusion.168
  765.6 8.8 fusion.157
  774.4 7.7 fusion.159
  783.7 5.9 fusion.166
  789.6 8.1 add_bitcast_fusion.3
  797.7 9.2 fusion.269
  806.9 95.0 %all-reduce.13.cloned.1.call-done = (bf16[1,1024,1536]{2,1,0:T(8,128)(2,1)}, bf16[1,1024,1536]{2,1,0:T(8,128)(2,1)}) async-done(((bf16[1,1024,1536]{2,1,0:T(8,128)(2,1)}, bf16[1,1024,1536]{2,1,0:T(8,128)(2,1)}), (bf16[1,1024,1536]{2,1,0:T(8,128)(2,1)}, bf16[1,1024,1536]{2,1,0:T(8,128)(2,1)})) %all-reduce.13.cloned.1.call-update) | async-done | bytes 6291472 | tf_op jit(solution)/shard_map/psum | solution.py:39
  909.8 1635.2 %all-reduce.11.cloned.1.call-done = (f32[1536,3,3,128]{0,3,2,1:T(8,128)}, f32[1536,3,3,128]{0,3,2,1:T(8,128)}, f32[3,128,1536]{2,1,0:T(8,128)}, f32[3,128,1536]{...) async-done(((f32[1536,3,3,128]{0,3,2,1:T(8,128)}, f32[1536,3,3,128]{0,3,2,1:T(8,128)}, ...) | async-done | bytes 56623120 | tf_op jit(solution)/shard_map/psum | solution.py:69
  2545.0 7.8 multiply_bitcast_fusion.4
  2559.8 12.4 pad_maximum_fusion.2
  2572.1 15.1 copy.52
  2587.2 4.7 multiply_bitcast_fusion.2
  2592.0 4.7 multiply_bitcast_fusion.3
  2596.7 7.2 pad_maximum_fusion
  2603.9 18.6 copy.53
  2632.1 6.7 pad_maximum_fusion.1
  2638.8 18.8 copy.54
  (216 shorter events, 94.0 us)
Async XLA Ops:
  7.2 197.1 %all-reduce.19.cloned.1.call-start = ((), (), s32[]{:S(2)}) async-start(), calls=%async_computation.4 | async-start | bytes 12582912 | tf_op jit(solution)/shard_map/psum | solution.py:18
  7.2 9.9 copy-start.16
  7.2 19.6 slice-start.4
  7.2 19.6 slice-start.12
  7.3 19.6 slice-start.13
  17.1 9.7 slice-start.5
  17.1 9.7 slice-start.14
  63.1 399.9 %all-reduce.17.cloned.1.call-start = ((), (), s32[]{:S(2)}) async-start(), calls=%async_computation.3 | async-start | bytes 12582912 | tf_op jit(solution)/shard_map/psum | solution.py:39
  63.4 21.0 slice-start.6
  63.4 20.9 slice-start.7
  63.4 20.9 slice-start.18
  63.4 20.9 slice-start.19
  73.3 11.1 slice-start.8
  73.3 11.1 slice-start.20
  73.3 26.1 slice-start
  84.4 6.9 copy-start.35
  84.4 15.0 slice-start.1
  99.9 14.2 slice-start.9
  104.6 9.5 slice-start.10
  204.3 7.2 copy-start.17
  211.5 8.5 slice-start.27
  213.3 6.7 slice-start.28
  213.3 6.7 slice-start.29
  261.7 11.0 slice-start.30
  265.9 6.8 slice-start.31
  265.9 6.8 slice-start.32
  265.9 6.7 copy-start.42
  324.2 8.8 copy-start.22
  324.2 8.8 copy-start.26
  324.2 8.8 copy-start.30
  340.7 305.1 %all-reduce.15.cloned.1.call-start = ((), (), s32[]{:S(2)}) async-start(), calls=%async_computation.2 | async-start | bytes 12582912 | tf_op jit(solution)/shard_map/psum | solution.py:18
  463.0 13.3 copy-start.8
  476.3 11.6 copy-start.36
  476.3 30.8 %slice-start.36 = ((s8[6291456]{0:T(1024)(128)(4,1)}), s8[4194304]{0:T(1024)(128)(4,1)S(1)}, s32[]{:S(2)}) async-start(s8[6291456]{0:T(1024)(128)(4,1)} %bitcast.512), calls=%async_computation.41 | async-start | bytes 8388608
  487.9 19.3 slice-start.15
  487.9 19.3 slice-start.16
  487.9 19.3 slice-start.37
  496.9 10.3 copy-start
  496.9 10.3 copy-start.6
  496.9 10.3 slice-start.17
  526.0 375.8 %all-reduce.13.cloned.1.call-start = ((), (), s32[]{:S(2)}) async-start(), calls=%async_computation.1 | async-start | bytes 12582912 | tf_op jit(solution)/shard_map/psum | solution.py:39
  526.1 11.7 copy-start.1
  526.1 11.7 copy-start.7
  645.8 8.3 copy-start.18
  654.1 9.5 copy-start.2
  654.1 9.5 slice-start.21
  656.0 7.6 slice-start.22
  656.0 7.6 slice-start.23
  656.0 7.6 copy-start.40
  685.7 19.4 copy-start.4
  705.2 10.0 slice-start.24
  708.4 6.8 slice-start.25
  708.5 6.8 slice-start.26
  708.5 6.7 copy-start.41
  765.6 8.8 copy-start.24
  765.6 8.8 copy-start.28
  765.6 8.8 copy-start.32
  782.1 1762.9 %all-reduce.11.cloned.1.call-start = ((), (), s32[]{:S(2)}) async-start(), calls=%async_computation | async-start | bytes 113246208 | tf_op jit(solution)/shard_map/psum | solution.py:69
  789.6 8.1 copy-start.3
  2545.0 11.0 slice-start.2
  2545.0 7.8 copy-start.11
  2545.0 9.4 copy-start.10
  2545.0 11.0 slice-start.3
  2638.8 18.8 copy-start.5
  (22 other events, 83.9 us)
Sparse Core Ops, SparseCore 0:
  63.2 122.1 all-reduce.18
  340.8 122.1 all-reduce.16
  526.2 119.6 all-reduce.14
  782.2 119.6 all-reduce.12
  908.0 1636.9 all-reduce.10
where the time goes:
time: 2680 us; the launch traced here: 2670 us
  waiting for transfers between devices  1920 us (72%)
  matrix products  584 us (22%)
  other arithmetic  87.6 us (3%)
  local copies, waits for them, and re-layouts  58.2 us (2%)
    psum x1, waiting for transfers between devices, device_backward(): lax.psum(grad_sum, data_axes) / replicas  1640 us
    psum x2, waiting for transfers between devices, layer_backward(): in_sum = lax.psum(in_part, 'tp')  193 us
    psum x2, waiting for transfers between devices, layer_backward(): mid_sum = lax.psum(mid_part, 'tp')  95 us
    dot_general x4, matrix products, layer_backward(): jnp.einsum('bnqk,bqnd->bknd', d_scores, queries, preferred_element_type=j...  77.5 us
    dot_general x4, matrix products, layer_backward(): jnp.einsum('bnqk,bknd->bqnd', d_scores, keys_all, preferred_element_type=...  76.9 us
    another operation x12, other arithmetic, device_backward(): jnp.stack([grad_set[slot_idx] for grad_set in grad_acc])  64.3 us
    unnamed x165, local copies, waits for them, and re-layouts  57.7 us
  transfers between devices with their start and end apart: 5, of which 4 were waited for; matrix products, arithmetic and copies ran while one was open for 8% of the time, Pallas kernels for 0%

commit v1 on v0

v1 whole, which is shorter than its diff:
```python
import functools

import jax
import jax.numpy as jnp
from jax import lax
from jax.experimental import pallas as pl
from jax.experimental.pallas import tpu as pltpu
from jax.sharding import PartitionSpec as P

F32, BF16 = jnp.float32, jnp.bfloat16
PLAIN = (((1,), (0,)), ((), ()))
BLOCK = 192
LANES = (((1,), (1,)), ((), ()))
ROWS = (((0,), (0,)), ((), ()))
ANY = pl.BlockSpec(memory_space=pl.ANY)
MESH = pl.DeviceIdType.MESH
TANH_1 = 0.7978845608028654
TANH_3 = 0.044715 * TANH_1
KINDS = DOWN, UP, QKV, OUT = range(4)
(
    START,
    LOAD_MLP,
    WAIT_MLP,
    LOAD_ATTN,
    WAIT_ATTN,
    LOAD_HEAD,
    ACT,
    MLP,
    PROJECT,
    HEAD,
    PART,
    SEND,
    PAIR,
    TOTAL,
    DONE,
    FREE,
    GRAD,
    MEAN,
    FINISH,
) = range(19)


def dot(a, b, dims=PLAIN):
    return lax.dot_general(a, b, dims, preferred_element_type=F32)


def aligned(i, n=16):
    return pl.multiple_of(i, n)


class Place:
    def __init__(self):
        self.iz, self.iy, self.tp = lax.axis_index("dpy"), lax.axis_index("dpx"), lax.axis_index("tp")
        self.core = self.tp % 2
        self.other_core = self.tp + 1 - 2 * self.core
        self.other_chip = self.tp + 2 - 4 * (self.tp // 2)
        self.inner = (self.iz == 1) | (self.iz == 2)
        self.outer = jnp.logical_not(self.inner)
        self.late = self.iz // 2
        self.fold = self.iz + 1 - 2 * (self.iz % 2)
        self.mid = 3 - self.iz


def signal(sem, axis, i):
    pl.semaphore_signal(sem, inc=1, device_id={axis: i}, device_id_type=MESH)


def entry_barrier(at):
    sem = pltpu.get_barrier_semaphore()
    signal(sem, "dpx", 1 - at.iy)
    signal(sem, "dpy", at.fold)
    signal(sem, "tp", at.other_core)
    signal(sem, "tp", at.other_chip)

    @pl.when(at.inner)
    def _():
        signal(sem, "dpy", at.mid)

    pl.semaphore_wait(sem, 4 + (at.iz + 1) // 2 - 2 * (at.iz // 3))


def in_place(rows, fn):
    n = next(b for b in (32, 16) if rows % b == 0)

    @pl.loop(0, rows // n)
    def _(i):
        fn(aligned(i * n, n), n)


class Combine:
    def __init__(self, wide, narrow, sem):
        self.wide, self.narrow, self.sem = wide, narrow, sem
        self.rows = wide.shape[0]

    def __call__(self, fn, ins, out):
        rows, cols = out.shape
        for lo in range(0, rows, self.rows):
            n = min(self.rows, rows - lo)
            part = lambda ref: ref.at[pl.ds(lo, n), :]
            narrow = [self.narrow.at[k, 0:n, 0:cols] for k in range(3)]
            mine = narrow.pop()
            bufs = [self.wide.at[0:n, 0:cols] if r.dtype == F32 else narrow.pop() for r in ins]
            loads = [pltpu.make_async_copy(part(r), b, self.sem.at[k]) for k, (r, b) in enumerate(zip(ins, bufs))]
            for c in loads:
                c.start()
            for c in loads:
                c.wait()

            def block(i, k):
                at = pl.ds(i, k)
                mine[at, :] = fn(*(b[at, :].astype(F32) for b in bufs)).astype(BF16)

            in_place(n, block)
            store = pltpu.make_async_copy(mine, part(out), self.sem.at[3])
            store.start()
            store.wait()


class Mean:
    steps = 6

    def __init__(self, at, combine, replicas, base, rows, first, g16, g32, fin, a_bufs, b_bufs, send, recv):
        self.at, self.combine, self.scale = at, combine, 1.0 / replicas
        self.g16, self.g32, self.fin = g16, g32, fin
        self.h, self.h2 = first // 2, (rows - first) // 2
        self.base, self.first = base, base + first
        self.r0, self.r1, self.r2, self.s1 = a_bufs
        if self.h2:
            self.b0, self.b1, self.b2, self.t1, self.t2 = b_bufs
        self.send, self.recv = send, recv

    def a(self, ref, own):
        start = self.base + (self.at.iy if own else 1 - self.at.iy) * self.h
        return ref.at[pl.ds(aligned(start), self.h), :]

    def b(self, ref, own, base):
        start = base + (self.at.late if own else 1 - self.at.late) * self.h2
        return ref.at[pl.ds(aligned(start), self.h2), :]

    def copy(self, k, src, dst, axis, to):
        return pltpu.make_async_remote_copy(
            src_ref=src, dst_ref=dst, send_sem=self.send.at[k], recv_sem=self.recv.at[k], device_id={axis: to}, device_id_type=MESH
        )

    def line(self, k):
        at, fin = self.at, self.fin
        if k == 0:
            return self.copy(k, self.a(self.g16, False), self.r0, "dpx", 1 - at.iy)
        if k == 1:
            return self.copy(k, self.s1, self.r1, "dpy", at.fold)
        if k == 2:
            return self.copy(k, self.s1, self.r2, "dpy", at.mid)
        if k == 3:
            return self.copy(k, self.a(fin, True), self.a(fin, True), "dpy", at.fold)
        if k == 4:
            return self.copy(k, self.a(fin, True), self.a(fin, True), "dpx", 1 - at.iy)
        if k in (5, 6):
            return self.copy(k, self.b(self.g16, k == 6, self.first), self.b(self.b0, k == 6, 0), "dpy", at.fold)
        if k == 7:
            return self.copy(k, self.t1, self.b1, "dpy", at.mid)
        if k == 8:
            return self.copy(k, self.t2, self.b2, "dpx", 1 - at.iy)
        if k == 9:
            return self.copy(k, self.b(fin, True, self.first), self.b(fin, True, self.first), "dpy", at.mid)
        own = k == 10
        return self.copy(k, self.b(fin, own, self.first), self.b(fin, own, self.first), "dpy", at.fold)

    def landed(self, k):
        self.line(k).wait_recv()

    def step(self, n):
        at, two = self.at, bool(self.h2)
        if n == 0:
            self.line(0).start()
            if two:

                @pl.when(at.outer)
                def _():
                    self.line(5).start()
                    self.line(6).start()

        elif n == 1:
            self.landed(0)

            @pl.when(at.outer)
            def _():
                self.combine(lambda g, r: g + r, [self.a(self.g32, True), self.r0], self.s1)
                self.line(1).start()

            if two:

                @pl.when(at.inner)
                def _():
                    self.landed(5)
                    self.combine(lambda g, r: g + r, [self.b(self.g32, False, self.first), self.b(self.b0, False, 0)], self.t1)
                    self.line(7).start()

        elif n == 2:

            @pl.when(at.inner)
            def _():
                self.landed(1)
                self.combine(lambda g, r, q: g + r + q, [self.a(self.g32, True), self.r0, self.r1], self.s1)
                self.line(2).start()
                if two:
                    self.landed(6)
                    self.landed(7)
                    own = [self.b(self.g32, True, self.first), self.b(self.b0, True, 0), self.b1]
                    self.combine(lambda g, r, q: g + r + q, own, self.t2)
                    self.line(8).start()

        elif n == 3:

            @pl.when(at.inner)
            def _():
                self.landed(2)
                self.combine(lambda s, r: (s + r) * self.scale, [self.s1, self.r2], self.a(self.fin, True))
                self.line(3).start()
                self.line(4).start()
                if two:
                    self.landed(8)
                    self.combine(lambda s, r: (s + r) * self.scale, [self.t2, self.b2], self.b(self.fin, True, self.first))
                    self.line(9).start()
                    self.line(10).start()

        elif n == 4:

            @pl.when(at.outer)
            def _():
                self.landed(3)
                self.line(4).start()

            if two:

                @pl.when(at.inner)
                def _():
                    self.landed(9)
                    self.line(11).start()

        else:
            self.landed(4)
            self.line(0).wait_send()
            self.line(4).wait_send()

            @pl.when(at.outer)
            def _():
                self.line(1).wait_send()
                if two:
                    self.landed(10)
                    self.landed(11)
                    self.line(5).wait_send()
                    self.line(6).wait_send()

            @pl.when(at.inner)
            def _():
                self.line(2).wait_send()
                self.line(3).wait_send()
                if two:
                    for k in (7, 8, 9, 10, 11):
                        self.line(k).wait_send()


class Backward:
    def __init__(self, dims, refs):
        self.__dict__.update(dims)
        self.at = Place()
        refs = list(refs)
        for name in self.names[0]:
            setattr(self, name, refs.pop(0))
        self.fins = [refs.pop(0) for _ in KINDS]
        self.tensors = [refs.pop(0) for _ in range(self.count)]
        for name, ref in zip(self.names[1], refs, strict=True):
            setattr(self, name, ref)
        self.half = self.s // 2
        self.blk = min(256, self.half)
        self.means, self.grads = {}, {}
        tensors, i = list(self.tensors), 0
        combine = Combine(self.wide, self.narrow, self.combine_sem)
        for l in range(self.layers):
            for kind in KINDS:
                parts, first = self.cuts[kind, l]
                g16, g32, a = tensors.pop(0), tensors.pop(0), tensors.pop(0)
                rows = g16.shape[0] // parts
                b0, b = (tensors.pop(0), tensors.pop(0)) if rows > first else (None, None)
                self.grads[kind, l] = g16, g32, rows
                for p in range(parts):
                    a_bufs = [a.at[p, j] for j in range(4)]
                    b_bufs = [b0.at[p]] + [b.at[p, j] for j in range(4)] if rows > first else None
                    sems = self.dp_send.at[i], self.dp_recv.at[i]
                    self.means[kind, l, p] = Mean(self.at, combine, self.replicas, p * rows, rows, first, g16, g32, self.fins[kind].at[l], a_bufs, b_bufs, *sems)
                    i += 1

    def local(self, k, src, dst):
        return pltpu.make_async_copy(src, dst, self.local_sem.at[k])

    def mlp_weights(self, l):
        return [self.local(0, self.w_up.at[l], self.wu_v), self.local(1, self.w_down.at[l], self.wd_v)]

    def attn_weights(self, l):
        d, heads = self.hd // self.heads, self.heads
        cols = [self.local(4 + c * heads + n, self.w_qkv.at[l, c, n], self.wq_v.at[:, pl.ds((c * heads + n) * d, d)]) for c in range(3) for n in range(heads)]
        rows = [self.local(4 + 3 * heads + n, self.w_out.at[l, n], self.wo_v.at[pl.ds(n * d, d), :]) for n in range(heads)]
        return cols + rows

    def top_grad(self, m):
        return self.local(2 + m, self.d_out.at[m], self.res.at[pl.ds(m * self.s, self.s), :])

    def mlp(self, l, m, own):
        half, blk, cols = self.half, self.blk, min(512, self.f)
        start = (self.at.core if own else 1 - self.at.core) * half
        part = (self.own if own else self.part).at[m]

        def body(step, y_ref, a_ref):
            i = step.index[0]
            rows = pl.ds(aligned(m * self.s + start + i * blk, blk), blk)
            y, g = y_ref[...], self.res[rows, :]
            for c in range(self.f // cols):
                sl = slice(c * cols, (c + 1) * cols)
                h = dot(y, self.wu_v[:, sl])
                da = dot(g, self.wd_v[sl, :], LANES)
                h2 = h * h
                t = jnp.tanh(h * (TANH_1 + TANH_3 * h2))
                cdf = 0.5 * t + 0.5
                slope = cdf + (0.5 * h) * (1.0 - t * t) * (TANH_1 + (3.0 * TANH_3) * h2)
                a_ref[:, sl] = (h * cdf).astype(BF16)
                self.dh_v[rows, sl] = (da * slope).astype(BF16)
            dh = self.dh_v[rows, :]
            wcols = min(512, self.w)
            for c in range(self.w // wcols):
                sl = slice(c * wcols, (c + 1) * wcols)
                part[pl.ds(aligned(i * blk, blk), blk), sl] = dot(dh, self.wu_v[sl, :], LANES).astype(BF16)

        row = lambda width: pl.BlockSpec((blk, width), lambda i: (i, 0))
        pltpu.emit_pipeline(body, grid=(half // blk,), in_specs=[row(self.w)], out_specs=[row(self.f)], _explicit_indices=True)(
            self.y_saved.at[l, m, pl.ds(aligned(start, blk), half), :], self.act.at[pl.ds(aligned(m * self.s + start, blk), half), :]
        )

    def qkv(self, l, m):
        blk, cols = self.blk, min(384, 3 * self.hd)

        def body(x_ref, out_ref):
            x = x_ref[...]
            for c in range(3 * self.hd // cols):
                sl = slice(c * cols, (c + 1) * cols)
                out_ref[:, sl] = dot(x, self.wq_v[:, sl]).astype(BF16)

        row = lambda width: pl.BlockSpec((blk, width), lambda i: (i, 0))
        pltpu.emit_pipeline(body, grid=(self.s // blk,), in_specs=[row(self.w)], out_specs=[row(3 * self.hd)])(
            self.x_saved.at[l, m], self.qkv_hbm.at[pl.ds(m * self.s, self.s), :]
        )

    def head_loads(self, m, n):
        d = self.hd // self.heads
        slot = (m * self.heads + n) % 2
        base = 4 + 4 * self.heads + 3 * slot
        return [
            self.local(base + c, self.qkv_hbm.at[pl.ds(m * self.s, self.s), pl.ds((c * self.heads + n) * d, d)], self.head.at[slot, c])
            for c in range(3)
        ]

    def attn(self, l, m, n):
        s, d, blk = self.s, self.hd // self.heads, min(256, self.s)
        scale = d**-0.5
        slot = (m * self.heads + n) % 2
        for c in self.head_loads(m, n):
            c.wait()
        if n + 1 < self.heads:
            for c in self.head_loads(m, n + 1):
                c.start()
        mine = slice(m * s, (m + 1) * s)
        col = slice(n * d, (n + 1) * d)
        q_ref, k_ref, v_ref = (self.head.at[slot, c] for c in range(3))
        p_ref, ds_ref = self.dh_v.at[0:s, 0:s], self.dh_v.at[s : 2 * s, 0:s]
        do_ref = self.do_v
        do_ref[...] = dot(self.res[mine, :], self.wo_v[col, :], LANES).astype(BF16)
        keys, vals = k_ref[...], v_ref[...]
        keys_t, vals_t = keys.T, vals.T
        place = lambda c: slice((c * self.heads + n) * d, (c * self.heads + n + 1) * d)
        block = lambda i: slice(i * blk, (i + 1) * blk)
        scores = lambda i: (dot(keys, q_ref[block(i), :], LANES), dot(vals, do_ref[block(i), :], LANES))
        ahead = scores(0)
        for i in range(s // blk):
            sc, dp = ahead
            if i + 1 < s // blk:
                ahead = scores(i + 1)
            sl = block(i)
            out = slice(m * s + i * blk, m * s + (i + 1) * blk)
            top = jnp.max(sc, axis=0, keepdims=True)
            e = jnp.exp((sc - top) * scale)
            inv = 1.0 / jnp.sum(e, axis=0, keepdims=True)
            row_dot = jnp.sum(dp * e, axis=0, keepdims=True) * inv
            pb = (e * inv).astype(BF16)
            ds = (e * ((dp - row_dot) * (inv * scale))).astype(BF16)
            p_ref[:, sl] = pb
            ds_ref[:, sl] = ds
            self.o_v[out, col] = dot(vals_t, pb).T.astype(BF16)
            self.dqkv_v[out, place(0)] = dot(keys_t, ds).T.astype(BF16)
        self.dqkv_v[mine, place(1)] = dot(ds_ref[...], q_ref[...]).astype(BF16)
        self.dqkv_v[mine, place(2)] = dot(p_ref[...], do_ref[...]).astype(BF16)

    def attn_part(self, l, m, own):
        half, cols = self.half, min(512, self.w)
        start = (self.at.core if own else 1 - self.at.core) * half
        part = (self.own if own else self.part).at[m]

        @pl.loop(0, half // self.blk)
        def _(i):
            dqkv = self.dqkv_v[pl.ds(aligned(m * self.s + start + i * self.blk, self.blk), self.blk), :]
            for c in range(self.w // cols):
                sl = slice(c * cols, (c + 1) * cols)
                part[pl.ds(aligned(i * self.blk, self.blk), self.blk), sl] = dot(dqkv, self.wq_v[sl, :], LANES).astype(BF16)

    def tp_copy(self, k, m, src, dst, to):
        return pltpu.make_async_remote_copy(
            src_ref=src, dst_ref=dst, send_sem=self.tp_send.at[k, m], recv_sem=self.tp_recv.at[k, m], device_id={"tp": to}, device_id_type=MESH
        )

    def tp_line(self, k, m):
        at = self.at
        if k == 0:
            return self.tp_copy(0, m, self.part.at[m], self.from_core.at[m], at.other_core)
        if k == 1:
            return self.tp_copy(1, m, self.own.at[m], self.from_chip.at[m], at.other_chip)
        rows = self.res.at[pl.ds(aligned(m * self.s + at.core * self.half), self.half), :]
        return self.tp_copy(2, m, rows, rows, at.other_core)

    def tp_pair(self, m, first):
        line = self.tp_line(0, m)
        line.wait_recv()
        own, got = self.own.at[m], self.from_core.at[m]

        def add(i, n):
            r = pl.ds(i, n)
            own[r, :] = (own[r, :].astype(F32) + got[r, :].astype(F32)).astype(BF16)

        in_place(self.half, add)
        line.wait_send()
        if not first:
            pl.semaphore_wait(self.chip_free.at[m], 1)
        self.tp_line(1, m).start()

    def tp_total(self, m, last, credit):
        line = self.tp_line(1, m)
        line.wait_recv()
        own, got = self.own.at[m], self.from_chip.at[m]
        base = m * self.s + self.at.core * self.half

        def add(i, n):
            r, b = pl.ds(i, n), pl.ds(aligned(base + i, n), n)
            self.res[b, :] = (self.res[b, :].astype(F32) + (own[r, :].astype(F32) + got[r, :].astype(F32))).astype(BF16)

        in_place(self.half, add)
        line.wait_send()
        if not last:
            signal(self.chip_free.at[m], "tp", self.at.other_chip)
        if credit:
            pl.semaphore_wait(self.core_free, 1)
        self.tp_line(2, m).start()

    def tp_done(self, m):
        line = self.tp_line(2, m)
        line.wait_recv()
        line.wait_send()

    def release_rows(self):
        signal(self.core_free, "tp", self.at.other_core)

    def grad(self, kind, l, part):
        rhs = (self.res, self.dh_v, self.dqkv_v, self.res)[kind]
        g16, g32, rows = self.grads[kind, l]
        cols = g32.shape[1]
        lo, hi = part * rows, (part + 1) * rows
        tile = next(t for t in (256, 384, 128) if rows % t == 0)
        chunk = min(512 if cols % 512 == 0 else 384, cols)
        two = self.mbs * self.s

        def put(lhs, o16_ref, o32_ref):
            for c in range(cols // chunk):
                sl = slice(c * chunk, (c + 1) * chunk)
                v = dot(lhs, rhs[:, sl], ROWS)
                o32_ref[:, sl] = v
                o16_ref[:, sl] = v.astype(BF16)

        out = pl.BlockSpec((tile, cols), lambda j: (j, 0))
        dst = (g16.at[lo:hi, :], g32.at[lo:hi, :])
        grid = ((hi - lo) // tile,)
        if kind == OUT:

            def body(step, *outs):
                put(self.o_v[:, pl.ds(aligned(lo + step.index[0] * tile, tile), tile)], *outs)

            pltpu.emit_pipeline(body, grid=grid, in_specs=[], out_specs=[out, out], _explicit_indices=True)(*dst)
            return
        if kind == DOWN:
            src, spec = self.act.at[:, lo:hi], pl.BlockSpec((two, tile), lambda j: (0, j))
        else:
            src = (self.y_saved if kind == UP else self.x_saved).at[l, :, :, lo:hi]
            spec = pl.BlockSpec((self.mbs, self.s, tile), lambda j: (0, 0, j))

        def body(lhs_ref, *outs):
            put(lhs_ref[...].reshape(two, tile), *outs)

        pltpu.emit_pipeline(body, grid=grid, in_specs=[spec], out_specs=[out, out])(src, *dst)


def run(b, order):
    for what, *rest in order:
        if what == START:
            for c in b.mlp_weights(b.layers - 1):
                c.start()
            for m in range(b.mbs):
                b.top_grad(m).start()
            for c in b.attn_weights(b.layers - 1):
                c.start()
            entry_barrier(b.at)
            for m in range(b.mbs):
                b.top_grad(m).wait()
        elif what in (LOAD_MLP, LOAD_ATTN, LOAD_HEAD):
            for c in {LOAD_MLP: b.mlp_weights, LOAD_ATTN: b.attn_weights, LOAD_HEAD: b.head_loads}[what](*rest):
                c.start()
        elif what in (WAIT_MLP, WAIT_ATTN):
            for c in {WAIT_MLP: b.mlp_weights, WAIT_ATTN: b.attn_weights}[what](*rest):
                c.wait()
        elif what == SEND:
            b.tp_line(0, rest[0]).start()
        elif what == MEAN:
            *which, n = rest
            b.means[tuple(which)].step(n)
        elif what == FINISH:
            out = [b.local(2 + m, b.res.at[pl.ds(m * b.s, b.s), :], b.d_in.at[m]) for m in range(b.mbs)]
            for c in out:
                c.start()
            for c in out:
                c.wait()
        else:
            part = {
                MLP: b.mlp,
                PROJECT: b.qkv,
                HEAD: b.attn,
                PART: b.attn_part,
                PAIR: b.tp_pair,
                TOTAL: b.tp_total,
                DONE: b.tp_done,
                FREE: b.release_rows,
                GRAD: b.grad,
            }[what]
            part(*rest)


def mega_kernel(dims, order, *refs):
    run(Backward(dims, refs), order)


def backward(x_saved, y_saved, d_out, w_qkv, w_out, w_up, w_down, replicas):
    layers, mbs, s, w = x_saved.shape
    f, heads, d = w_up.shape[2], w_qkv.shape[2], w_qkv.shape[4]
    hd, rows = heads * d, mbs * s
    half = s // 2
    shapes = (f, w), (w, f), (w, 3 * hd), (hd, w)
    hbm = {"d_in": (mbs, s, w), "act": (rows, f), "qkv_hbm": (rows, 3 * hd)}
    fins = [(layers, *shape) for shape in shapes]
    cuts, tensors = {}, []
    for l in range(layers):
        for k in KINDS:
            r, c = shapes[k]
            parts, share = CUTS[l][k]
            n = r // parts
            first = round(n * share / 32) * 32
            cuts[k, l] = parts, first
            tensors += [((r, c), BF16), ((r, c), F32), ((parts, 4, first // 2, c), BF16)]
            if n > first:
                tensors += [((parts, n - first, c), BF16), ((parts, 4, (n - first) // 2, c), BF16)]
    vmem = {
        "wu_v": (w, f),
        "wd_v": (f, w),
        "wq_v": (w, 3 * hd),
        "wo_v": (hd, w),
        "res": (rows, w),
        "dh_v": (rows, f),
        "dqkv_v": (rows, 3 * hd),
        "o_v": (rows, hd),
        "part": (mbs, half, w),
        "own": (mbs, half, w),
        "from_core": (mbs, half, w),
        "from_chip": (mbs, half, w),
        "head": (2, 3, s, d),
        "do_v": (s, d),
        "narrow": (3, min(BLOCK, w // 2), w),
    }
    n = sum(parts for parts, _ in cuts.values())
    dma, regular = pltpu.SemaphoreType.DMA, pltpu.SemaphoreType.REGULAR
    sems = {
        "dp_send": dma((n, 12)),
        "dp_recv": dma((n, 12)),
        "tp_send": dma((3, mbs)),
        "tp_recv": dma((3, mbs)),
        "local_sem": dma((4 + 4 * heads + 6,)),
        "chip_free": regular((mbs,)),
        "core_free": regular,
        "combine_sem": dma((4,)),
        "wide": pltpu.VMEM((min(BLOCK, w // 2), w), F32),
    }
    ins = ("x_saved", "y_saved", "d_out", "w_qkv", "w_out", "w_up", "w_down")
    names = ((*ins, *hbm), (*vmem, *sems))
    dims = dict(names=names, count=len(tensors), layers=layers, mbs=mbs, s=s, w=w, f=f, heads=heads, hd=hd, replicas=replicas, cuts=cuts)
    outs = [(v, BF16) for v in (*hbm.values(), *fins)] + tensors
    outs = pl.pallas_call(
        functools.partial(mega_kernel, dims, ORDER),
        in_specs=[ANY] * len(ins),
        out_specs=[ANY] * len(outs),
        out_shape=[jax.ShapeDtypeStruct(*v) for v in outs],
        scratch_shapes=[pltpu.VMEM(v, BF16) for v in vmem.values()] + list(sems.values()),
        compiler_params=pltpu.CompilerParams(collective_id=0, has_side_effects=True, vmem_limit_bytes=67043328),
        name="backward",
    )(x_saved, y_saved, d_out, w_qkv, w_out, w_up, w_down)
    return outs[0], *outs[len(hbm) : len(hbm) + len(fins)]


def widen(a, pieces=0):
    layers, r, c = a.shape
    blk = min(512 if r % 512 == 0 else 384, r)
    src = pl.BlockSpec((None, blk, c), lambda l, i: (l, i, 0))
    if not pieces:
        dst, shape = src, (layers, r, c)
    else:
        dst, shape = pl.BlockSpec((None, pieces, blk, c // pieces), lambda l, i: (l, 0, i, 0)), (layers, pieces, r, c // pieces)

    def body(a_ref, o_ref):
        if not pieces:
            o_ref[...] = a_ref[...].astype(F32)
            return
        n = c // pieces
        for j in range(pieces):
            o_ref[j] = a_ref[:, j * n : (j + 1) * n].astype(F32)

    return pl.pallas_call(
        body, grid=(layers, r // blk), in_specs=[src], out_specs=dst, out_shape=jax.ShapeDtypeStruct(shape, F32), name="widen"
    )(a)


CUTS = (
    ((1, 0.5), (1, 0.5), (1, 0.5), (1, 1.0)),
    ((1, 0.5), (1, 0.5), (1, 0.5), (1, 1.0)),
)
ORDER = (
    (START,), (WAIT_MLP, 1), (MLP, 1, 0, False), (SEND, 0), (MLP, 1, 0, True), (PAIR, 0, True), (MLP, 1, 1, False), (SEND, 1),
    (MLP, 1, 1, True), (LOAD_MLP, 0), (PAIR, 1, True), (GRAD, DOWN, 1, 0), (FREE,), (MEAN, DOWN, 1, 0, 0), (GRAD, UP, 1, 0),
    (MEAN, UP, 1, 0, 0), (TOTAL, 0, False, True), (WAIT_ATTN, 1), (PROJECT, 1, 0), (PROJECT, 1, 1), (DONE, 0), (LOAD_HEAD, 0, 0),
    (HEAD, 1, 0, 0), (MEAN, DOWN, 1, 0, 1), (TOTAL, 1, False, False), (HEAD, 1, 0, 1), (DONE, 1), (HEAD, 1, 0, 2), (PART, 1, 0, False),
    (SEND, 0), (PART, 1, 0, True), (LOAD_HEAD, 1, 0), (HEAD, 1, 1, 0), (PAIR, 0, False), (HEAD, 1, 1, 1), (HEAD, 1, 1, 2), (MEAN, UP, 1, 0, 1),
    (PART, 1, 1, False), (SEND, 1), (PART, 1, 1, True), (LOAD_ATTN, 0), (GRAD, OUT, 1, 0), (FREE,), (MEAN, OUT, 1, 0, 0), (PAIR, 1, False),
    (GRAD, QKV, 1, 0), (MEAN, QKV, 1, 0, 0), (TOTAL, 0, False, True), (WAIT_ATTN, 0), (PROJECT, 0, 0), (MEAN, OUT, 1, 0, 1), (DONE, 0),
    (WAIT_MLP, 0), (MLP, 0, 0, False), (SEND, 0), (MLP, 0, 0, True), (PAIR, 0, False), (MEAN, DOWN, 1, 0, 2), (TOTAL, 1, False, False),
    (PROJECT, 0, 1), (DONE, 1), (MLP, 0, 1, False), (SEND, 1), (MEAN, UP, 1, 0, 2), (MLP, 0, 1, True), (PAIR, 1, False), (MEAN, DOWN, 1, 0, 3),
    (MEAN, QKV, 1, 0, 1), (GRAD, DOWN, 0, 0), (FREE,), (MEAN, DOWN, 0, 0, 0), (TOTAL, 0, False, True), (MEAN, UP, 1, 0, 3), (DONE, 0),
    (MEAN, OUT, 1, 0, 2), (GRAD, UP, 0, 0), (MEAN, UP, 0, 0, 0), (MEAN, DOWN, 1, 0, 4), (TOTAL, 1, False, False), (LOAD_HEAD, 0, 0),
    (HEAD, 0, 0, 0), (DONE, 1), (HEAD, 0, 0, 1), (MEAN, QKV, 1, 0, 2), (HEAD, 0, 0, 2), (MEAN, DOWN, 0, 0, 1), (PART, 0, 0, False), (SEND, 0),
    (PART, 0, 0, True), (LOAD_HEAD, 1, 0), (HEAD, 0, 1, 0), (MEAN, UP, 1, 0, 4), (PAIR, 0, False), (HEAD, 0, 1, 1), (MEAN, OUT, 1, 0, 3),
    (HEAD, 0, 1, 2), (PART, 0, 1, False), (SEND, 1), (PART, 0, 1, True), (GRAD, OUT, 0, 0), (FREE,), (MEAN, OUT, 0, 0, 0), (PAIR, 1, False),
    (GRAD, QKV, 0, 0), (MEAN, QKV, 0, 0, 0), (TOTAL, 0, True, True), (MEAN, UP, 0, 0, 1), (DONE, 0), (MEAN, QKV, 1, 0, 3),
    (TOTAL, 1, True, False), (MEAN, OUT, 0, 0, 1), (MEAN, OUT, 1, 0, 4), (DONE, 1), (FINISH,), (MEAN, DOWN, 0, 0, 2), (MEAN, QKV, 1, 0, 4),
    (MEAN, QKV, 0, 0, 1), (MEAN, DOWN, 0, 0, 3), (MEAN, UP, 0, 0, 2), (MEAN, OUT, 0, 0, 2), (MEAN, DOWN, 0, 0, 4), (MEAN, QKV, 0, 0, 2),
    (MEAN, UP, 0, 0, 3), (MEAN, OUT, 0, 0, 3), (MEAN, QKV, 0, 0, 3), (MEAN, UP, 0, 0, 4), (MEAN, OUT, 0, 0, 4), (MEAN, QKV, 0, 0, 4),
    (MEAN, DOWN, 1, 0, 5), (MEAN, UP, 1, 0, 5), (MEAN, OUT, 1, 0, 5), (MEAN, QKV, 1, 0, 5), (MEAN, DOWN, 0, 0, 5), (MEAN, OUT, 0, 0, 5),
    (MEAN, UP, 0, 0, 5), (MEAN, QKV, 0, 0, 5),
)


def solution(mesh):
    replicas = mesh.shape["dpy"] * mesh.shape["dpx"]
    data_axes = ("dpy", "dpx")
    act_spec = P(None, data_axes, None, None)
    tok_spec = P(data_axes, None, None)
    qkv_spec = P(None, None, None, "tp", None)
    wout_spec = P(None, "tp", None, None)
    up_spec = P(None, None, "tp")
    down_spec = P(None, "tp", None)

    def device_backward(x_saved, y_saved, d_out, w_qkv, w_out, w_up, w_down):
        layers, width, _, heads, d = w_qkv.shape
        by_head = jnp.transpose(w_qkv, (0, 2, 3, 1, 4))
        d_in, down, up, qkv, out = backward(x_saved, y_saved, d_out, by_head, w_out, w_up, w_down, replicas)
        g_qkv = jnp.transpose(widen(qkv, 3 * heads).reshape(layers, 3, heads, width, d), (0, 3, 1, 2, 4))
        g_out = widen(out).reshape(w_out.shape)
        return d_in, g_qkv, g_out, widen(up), widen(down)

    return jax.shard_map(
        device_backward,
        mesh=mesh,
        in_specs=(act_spec, act_spec, tok_spec, qkv_spec, wout_spec, up_spec, down_spec),
        out_specs=(tok_spec, qkv_spec, wout_spec, up_spec, down_spec),
        check_vma=False,
    )
```

time: 2680 us -> 756 us (0.28)
  waiting for transfers between devices: 1920 us -> 0 us
  Pallas kernels: 0 us -> 739 us
  matrix products: 584 us -> 0 us
  other arithmetic: 87.6 us -> 0 us
  local copies, waits for them, and re-layouts: 58.2 us -> 5.89 us
    psum x5 -> x0, waiting for transfers between devices: 1920 us -> none  [the longest x1 1640 us: device_backward(): lax.psum(grad_sum, data_axes) / replicas]
    pallas_call x0 -> x5, Pallas kernels: none -> 739 us  [the longest x1 704 us: backward(): pl.pallas_call(functools.partial(mega_kernel, dims, ORDER), in_specs=[ANY...]
    dot_general x64 -> x0, matrix products: 542 us -> none  [the longest x4 77.5 us: layer_backward(): jnp.einsum('bnqk,bqnd->bknd', d_scores, queries, preferred_element_type=j...]
    another operation x12 -> x0, other arithmetic: 64.3 us -> none  [device_backward(): jnp.stack([grad_set[slot_idx] for grad_set in grad_acc])]
    unnamed x165 -> x1, local copies, waits for them, and re-layouts: 57.7 us -> 5.89 us
    sub x4 -> x0, matrix products: 41.8 us -> none  [layer_backward(): probs_f = jax.nn.softmax(scores, axis=-1)]
  transfers between devices with their start and end apart: 5 -> 0, of which waited for: 4 -> 0; matrix products, arithmetic and copies ran while one was open for 8% -> 0% of each run, Pallas kernels for 0% -> 0%
where the time goes in v1:
time: 756 us; the launch traced here: 745 us
  Pallas kernels  739 us (98%)
    pallas_call x1, Pallas kernels, backward(): pl.pallas_call(functools.partial(mega_kernel, dims, ORDER), in_specs=[ANY...  704 us
    pallas_call x4, Pallas kernels, widen(): pl.pallas_call(body, grid=(layers, r // blk), in_specs=[src], out_specs=d...  34.7 us

profile of v1, /device:TPU:0, one launch (start us, length us, event | category | flops | bytes accessed | tf_op | source)
XLA Modules:
  0.0 745.5 jit_solution(13659599714807015947)
XLA Ops:
  0.6 704.0 %backward.1 = (bf16[2,1024,1536]{2,1,0:T(8,128)(2,1)}, bf16[2048,1536]{1,0:T(8,128)(2,1)}, bf16[2048,1152]{1,0:T(8,128)(2,1)}, bf16[2,1536,1536]{2,1,0:T(8,128)(...) custom-call(bf16[2,2,1024,1536]{3,2,1,0:T(8,128)(2,1)} %refs_0_.1, ...), custom_call_target="tpu_custom_call" | custom-call | tf_op jit(solution)/shard_map/backward/pallas_call | solution.py:607
  704.7 3.6 widen.5
  708.3 8.9 %widen.4 = f32[2,9,1536,128]{3,2,1,0:T(8,128)} custom-call(bf16[2,1536,1152]{2,1,0:T(8,128)(2,1)} %get-tuple-element.11.a_ref), custom_call_target="tpu_custom_call" | custom-call | tf_op jit(solution)/shard_map/widen/pallas_call | solution.py:636
  717.2 11.1 %widen.6 = f32[2,1536,1536]{2,1,0:T(8,128)} custom-call(bf16[2,1536,1536]{2,1,0:T(8,128)(2,1)} %get-tuple-element.13.a_ref), custom_call_target="tpu_custom_call" | custom-call | tf_op jit(solution)/shard_map/widen/pallas_call | solution.py:636
  728.3 11.1 %widen.7 = f32[2,1536,1536]{2,1,0:T(8,128)} custom-call(bf16[2,1536,1536]{2,1,0:T(8,128)(2,1)} %get-tuple-element.14.a_ref), custom_call_target="tpu_custom_call" | custom-call | tf_op jit(solution)/shard_map/widen/pallas_call | solution.py:636
  739.4 5.9 copy.13

commit v2 on v1

--- a/solution.py
+++ b/solution.py
@@ -9,7 +9,7 @@
 
 F32, BF16 = jnp.float32, jnp.bfloat16
 PLAIN = (((1,), (0,)), ((), ()))
-BLOCK = 192
+BLOCK = 128
 LANES = (((1,), (1,)), ((), ()))
 ROWS = (((0,), (0,)), ((), ()))
 ANY = pl.BlockSpec(memory_space=pl.ANY)
@@ -80,7 +80,7 @@
 
 
 def in_place(rows, fn):
-    n = next(b for b in (32, 16) if rows % b == 0)
+    n = next(b for b in (64, 48, 32, 16) if rows % b == 0)
 
     @pl.loop(0, rows // n)
     def _(i):
@@ -90,30 +90,41 @@
 class Combine:
     def __init__(self, wide, narrow, sem):
         self.wide, self.narrow, self.sem = wide, narrow, sem
-        self.rows = wide.shape[0]
+        self.rows = wide.shape[1]
 
     def __call__(self, fn, ins, out):
         rows, cols = out.shape
-        for lo in range(0, rows, self.rows):
-            n = min(self.rows, rows - lo)
+        pieces = [(lo, min(self.rows, rows - lo)) for lo in range(0, rows, self.rows)]
+        loads, bufs, stores = [], [], []
+        for k, (lo, n) in enumerate(pieces):
+            slot = k % 2
+            narrow = [self.narrow.at[slot, b, 0:n, 0:cols] for b in range(3)]
+            mine = narrow.pop()
+            here = [self.wide.at[slot, 0:n, 0:cols] if r.dtype == F32 else narrow.pop() for r in ins]
             part = lambda ref: ref.at[pl.ds(lo, n), :]
-            narrow = [self.narrow.at[k, 0:n, 0:cols] for k in range(3)]
-            mine = narrow.pop()
-            bufs = [self.wide.at[0:n, 0:cols] if r.dtype == F32 else narrow.pop() for r in ins]
-            loads = [pltpu.make_async_copy(part(r), b, self.sem.at[k]) for k, (r, b) in enumerate(zip(ins, bufs))]
-            for c in loads:
-                c.start()
-            for c in loads:
+            loads.append([pltpu.make_async_copy(part(r), b, self.sem.at[slot, q]) for q, (r, b) in enumerate(zip(ins, here))])
+            bufs.append((here, mine))
+            stores.append(pltpu.make_async_copy(mine, part(out), self.sem.at[slot, 3]))
+        for c in loads[0]:
+            c.start()
+        for k, (lo, n) in enumerate(pieces):
+            if k + 1 < len(pieces):
+                for c in loads[k + 1]:
+                    c.start()
+            for c in loads[k]:
                 c.wait()
-
-            def block(i, k):
-                at = pl.ds(i, k)
-                mine[at, :] = fn(*(b[at, :].astype(F32) for b in bufs)).astype(BF16)
+            if k >= 2:
+                stores[k - 2].wait()
+            here, mine = bufs[k]
+
+            def block(i, size, here=here, mine=mine):
+                at = pl.ds(i, size)
+                mine[at, :] = fn(*(b[at, :].astype(F32) for b in here)).astype(BF16)
 
             in_place(n, block)
-            store = pltpu.make_async_copy(mine, part(out), self.sem.at[3])
-            store.start()
-            store.wait()
+            stores[k].start()
+        for c in stores[-2:]:
+            c.wait()
 
 
 class Mean:
@@ -264,6 +275,7 @@
     def __init__(self, dims, refs):
         self.__dict__.update(dims)
         self.at = Place()
+        self.early = {entry[1] for entry in ORDER if entry[0] == ACT}
         refs = list(refs)
         for name in self.names[0]:
             setattr(self, name, refs.pop(0))
@@ -305,12 +317,28 @@
     def top_grad(self, m):
         return self.local(2 + m, self.d_out.at[m], self.res.at[pl.ds(m * self.s, self.s), :])
 
+    def act_only(self, l, m):
+        blk, cols = self.blk, min(512, self.f)
+
+        def body(y_ref, a_ref):
+            y = y_ref[...]
+            for c in range(self.f // cols):
+                sl = slice(c * cols, (c + 1) * cols)
+                h = dot(y, self.wu_v[:, sl])
+                t = jnp.tanh(h * (TANH_1 + TANH_3 * (h * h)))
+                a_ref[:, sl] = (h * (0.5 * t + 0.5)).astype(BF16)
+
+        row = lambda width: pl.BlockSpec((blk, width), lambda i: (i, 0))
+        pltpu.emit_pipeline(body, grid=(self.s // blk,), in_specs=[row(self.w)], out_specs=[row(self.f)])(
+            self.y_saved.at[l, m], self.act.at[pl.ds(m * self.s, self.s), :]
+        )
+
     def mlp(self, l, m, own):
         half, blk, cols = self.half, self.blk, min(512, self.f)
         start = (self.at.core if own else 1 - self.at.core) * half
         part = (self.own if own else self.part).at[m]
 
-        def body(step, y_ref, a_ref):
+        def body(step, y_ref, *a_ref):
             i = step.index[0]
             rows = pl.ds(aligned(m * self.s + start + i * blk, blk), blk)
             y, g = y_ref[...], self.res[rows, :]
@@ -322,7 +350,8 @@
                 t = jnp.tanh(h * (TANH_1 + TANH_3 * h2))
                 cdf = 0.5 * t + 0.5
                 slope = cdf + (0.5 * h) * (1.0 - t * t) * (TANH_1 + (3.0 * TANH_3) * h2)
-                a_ref[:, sl] = (h * cdf).astype(BF16)
+                for a in a_ref:
+                    a[:, sl] = (h * cdf).astype(BF16)
                 self.dh_v[rows, sl] = (da * slope).astype(BF16)
             dh = self.dh_v[rows, :]
             wcols = min(512, self.w)
@@ -331,8 +360,9 @@
                 part[pl.ds(aligned(i * blk, blk), blk), sl] = dot(dh, self.wu_v[sl, :], LANES).astype(BF16)
 
         row = lambda width: pl.BlockSpec((blk, width), lambda i: (i, 0))
-        pltpu.emit_pipeline(body, grid=(half // blk,), in_specs=[row(self.w)], out_specs=[row(self.f)], _explicit_indices=True)(
-            self.y_saved.at[l, m, pl.ds(aligned(start, blk), half), :], self.act.at[pl.ds(aligned(m * self.s + start, blk), half), :]
+        outs = [] if l in self.early else [self.act.at[pl.ds(aligned(m * self.s + start, blk), half), :]]
+        pltpu.emit_pipeline(body, grid=(half // blk,), in_specs=[row(self.w)], out_specs=[row(self.f)] * len(outs), _explicit_indices=True)(
+            self.y_saved.at[l, m, pl.ds(aligned(start, blk), half), :], *outs
         )
 
     def qkv(self, l, m):
@@ -506,20 +536,23 @@
 def run(b, order):
     for what, *rest in order:
         if what == START:
-            for c in b.mlp_weights(b.layers - 1):
+            up, down = b.mlp_weights(b.layers - 1)
+            up.start()
+            entry_barrier(b.at)
+            up.wait()
+            for c in [b.top_grad(m) for m in range(b.mbs)] + [down] + b.attn_weights(b.layers - 1):
                 c.start()
-            for m in range(b.mbs):
-                b.top_grad(m).start()
-            for c in b.attn_weights(b.layers - 1):
-                c.start()
-            entry_barrier(b.at)
-            for m in range(b.mbs):
-                b.top_grad(m).wait()
+            waiting = [b.top_grad(m) for m in range(b.mbs)]
         elif what in (LOAD_MLP, LOAD_ATTN, LOAD_HEAD):
             for c in {LOAD_MLP: b.mlp_weights, LOAD_ATTN: b.attn_weights, LOAD_HEAD: b.head_loads}[what](*rest):
                 c.start()
-        elif what in (WAIT_MLP, WAIT_ATTN):
-            for c in {WAIT_MLP: b.mlp_weights, WAIT_ATTN: b.attn_weights}[what](*rest):
+        elif what == WAIT_MLP:
+            up, down = b.mlp_weights(*rest)
+            if rest[0] < b.layers - 1:
+                up.wait()
+            down.wait()
+        elif what == WAIT_ATTN:
+            for c in b.attn_weights(*rest):
                 c.wait()
         elif what == SEND:
             b.tp_line(0, rest[0]).start()
@@ -533,7 +566,11 @@
             for c in out:
                 c.wait()
         else:
+            if what in (MLP, GRAD):
+                while waiting:
+                    waiting.pop().wait()
             part = {
+                ACT: b.act_only,
                 MLP: b.mlp,
                 PROJECT: b.qkv,
                 HEAD: b.attn,
@@ -585,7 +622,7 @@
         "from_chip": (mbs, half, w),
         "head": (2, 3, s, d),
         "do_v": (s, d),
-        "narrow": (3, min(BLOCK, w // 2), w),
+        "narrow": (2, 3, min(BLOCK, w // 2), w),
     }
     n = sum(parts for parts, _ in cuts.values())
     dma, regular = pltpu.SemaphoreType.DMA, pltpu.SemaphoreType.REGULAR
@@ -597,8 +634,8 @@
         "local_sem": dma((4 + 4 * heads + 6,)),
         "chip_free": regular((mbs,)),
         "core_free": regular,
-        "combine_sem": dma((4,)),
-        "wide": pltpu.VMEM((min(BLOCK, w // 2), w), F32),
+        "combine_sem": dma((2, 4)),
+        "wide": pltpu.VMEM((2, min(BLOCK, w // 2), w), F32),
     }
     ins = ("x_saved", "y_saved", "d_out", "w_qkv", "w_out", "w_up", "w_down")
     names = ((*ins, *hbm), (*vmem, *sems))
@@ -616,53 +653,109 @@
     return outs[0], *outs[len(hbm) : len(hbm) + len(fins)]
 
 
-def widen(a, pieces=0):
-    layers, r, c = a.shape
-    blk = min(512 if r % 512 == 0 else 384, r)
-    src = pl.BlockSpec((None, blk, c), lambda l, i: (l, i, 0))
-    if not pieces:
-        dst, shape = src, (layers, r, c)
-    else:
-        dst, shape = pl.BlockSpec((None, pieces, blk, c // pieces), lambda l, i: (l, 0, i, 0)), (layers, pieces, r, c // pieces)
-
-    def body(a_ref, o_ref):
-        if not pieces:
-            o_ref[...] = a_ref[...].astype(F32)
-            return
-        n = c // pieces
-        for j in range(pieces):
-            o_ref[j] = a_ref[:, j * n : (j + 1) * n].astype(F32)
-
+def finish_kernel(jobs, *refs):
+    n = len({job[0] for job in jobs})
+    ins, outs = refs[:n], refs[n : 2 * n]
+    narrow, wide, in_sem, out_sem = refs[2 * n :]
+    depth = narrow.shape[0]
+
+    def load(k):
+        which, l, lo, rows, _ = jobs[k]
+        src = ins[which].at[l, pl.ds(lo, rows), :]
+        return pltpu.make_async_copy(src, narrow.at[k % depth, 0:rows, 0 : src.shape[1]], in_sem.at[k % depth])
+
+    def store(k):
+        which, l, lo, rows, pieces = jobs[k]
+        cols = ins[which].shape[2]
+        if pieces:
+            src, dst = wide.at[k % depth, 0:rows, 0:cols], outs[which]
+            width = cols // pieces
+            return [
+                pltpu.make_async_copy(src.at[:, pl.ds(p * width, width)], dst.at[l, p, pl.ds(lo, rows), :], out_sem.at[k % depth, p])
+                for p in range(pieces)
+            ]
+        return [pltpu.make_async_copy(narrow.at[k % depth, 0:rows, 0:cols], outs[which].at[l, pl.ds(lo, rows), :], out_sem.at[k % depth, 0])]
+
+    ahead = depth // 2
+    for k in range(ahead):
+        load(k).start()
+    for k, (which, l, lo, rows, pieces) in enumerate(jobs):
+        if k + ahead < len(jobs):
+            if k + ahead >= depth:
+                for c in store(k + ahead - depth):
+                    c.wait()
+            load(k + ahead).start()
+        load(k).wait()
+        if pieces:
+            src, dst = narrow.at[k % depth], wide.at[k % depth]
+            cols = ins[which].shape[2]
+
+            def block(i, size):
+                dst[pl.ds(i, size), 0:cols] = src[pl.ds(i, size), 0:cols].astype(F32)
+
+            in_place(rows, block)
+        for c in store(k):
+            c.start()
+    for k in range(len(jobs) - depth, len(jobs)):
+        for c in store(k):
+            c.wait()
+
+
+def finish(d_in, fins, heads):
+    ins = (d_in, *fins)
+    pieces = (0, 1, 1, 3 * heads, 1)
+    jobs = []
+    for which, a in enumerate(ins):
+        layers, r, c = a.shape
+        blk = next(b for b in (256, 192, 128) if r % b == 0)
+        jobs += [(which, l, lo, blk, pieces[which]) for l in range(layers) for lo in range(0, r, blk)]
+    out = lambda a, p: jax.ShapeDtypeStruct(a.shape if not p else (a.shape[0], p, a.shape[1], a.shape[2] // p), F32 if p else BF16)
+    depth, width = 4, max(a.shape[2] for a in ins)
     return pl.pallas_call(
-        body, grid=(layers, r // blk), in_specs=[src], out_specs=dst, out_shape=jax.ShapeDtypeStruct(shape, F32), name="widen"
-    )(a)
+        functools.partial(finish_kernel, jobs),
+        in_specs=[ANY] * len(ins),
+        out_specs=[ANY] * len(ins),
+        out_shape=[out(a, p) for a, p in zip(ins, pieces)],
+        scratch_shapes=[
+            pltpu.VMEM((depth, 256, width), BF16),
+            pltpu.VMEM((depth, 256, width), F32),
+            pltpu.SemaphoreType.DMA((depth,)),
+            pltpu.SemaphoreType.DMA((depth, 3 * heads)),
+        ],
+        name="finish",
+    )(*ins)
 
 
 CUTS = (
-    ((1, 0.5), (1, 0.5), (1, 0.5), (1, 1.0)),
+    ((3, 0.5833), (2, 1.0), (2, 0.6667), (1, 1.0)),
     ((1, 0.5), (1, 0.5), (1, 0.5), (1, 1.0)),
 )
 ORDER = (
-    (START,), (WAIT_MLP, 1), (MLP, 1, 0, False), (SEND, 0), (MLP, 1, 0, True), (PAIR, 0, True), (MLP, 1, 1, False), (SEND, 1),
-    (MLP, 1, 1, True), (LOAD_MLP, 0), (PAIR, 1, True), (GRAD, DOWN, 1, 0), (FREE,), (MEAN, DOWN, 1, 0, 0), (GRAD, UP, 1, 0),
-    (MEAN, UP, 1, 0, 0), (TOTAL, 0, False, True), (WAIT_ATTN, 1), (PROJECT, 1, 0), (PROJECT, 1, 1), (DONE, 0), (LOAD_HEAD, 0, 0),
-    (HEAD, 1, 0, 0), (MEAN, DOWN, 1, 0, 1), (TOTAL, 1, False, False), (HEAD, 1, 0, 1), (DONE, 1), (HEAD, 1, 0, 2), (PART, 1, 0, False),
-    (SEND, 0), (PART, 1, 0, True), (LOAD_HEAD, 1, 0), (HEAD, 1, 1, 0), (PAIR, 0, False), (HEAD, 1, 1, 1), (HEAD, 1, 1, 2), (MEAN, UP, 1, 0, 1),
-    (PART, 1, 1, False), (SEND, 1), (PART, 1, 1, True), (LOAD_ATTN, 0), (GRAD, OUT, 1, 0), (FREE,), (MEAN, OUT, 1, 0, 0), (PAIR, 1, False),
-    (GRAD, QKV, 1, 0), (MEAN, QKV, 1, 0, 0), (TOTAL, 0, False, True), (WAIT_ATTN, 0), (PROJECT, 0, 0), (MEAN, OUT, 1, 0, 1), (DONE, 0),
-    (WAIT_MLP, 0), (MLP, 0, 0, False), (SEND, 0), (MLP, 0, 0, True), (PAIR, 0, False), (MEAN, DOWN, 1, 0, 2), (TOTAL, 1, False, False),
-    (PROJECT, 0, 1), (DONE, 1), (MLP, 0, 1, False), (SEND, 1), (MEAN, UP, 1, 0, 2), (MLP, 0, 1, True), (PAIR, 1, False), (MEAN, DOWN, 1, 0, 3),
-    (MEAN, QKV, 1, 0, 1), (GRAD, DOWN, 0, 0), (FREE,), (MEAN, DOWN, 0, 0, 0), (TOTAL, 0, False, True), (MEAN, UP, 1, 0, 3), (DONE, 0),
-    (MEAN, OUT, 1, 0, 2), (GRAD, UP, 0, 0), (MEAN, UP, 0, 0, 0), (MEAN, DOWN, 1, 0, 4), (TOTAL, 1, False, False), (LOAD_HEAD, 0, 0),
-    (HEAD, 0, 0, 0), (DONE, 1), (HEAD, 0, 0, 1), (MEAN, QKV, 1, 0, 2), (HEAD, 0, 0, 2), (MEAN, DOWN, 0, 0, 1), (PART, 0, 0, False), (SEND, 0),
-    (PART, 0, 0, True), (LOAD_HEAD, 1, 0), (HEAD, 0, 1, 0), (MEAN, UP, 1, 0, 4), (PAIR, 0, False), (HEAD, 0, 1, 1), (MEAN, OUT, 1, 0, 3),
-    (HEAD, 0, 1, 2), (PART, 0, 1, False), (SEND, 1), (PART, 0, 1, True), (GRAD, OUT, 0, 0), (FREE,), (MEAN, OUT, 0, 0, 0), (PAIR, 1, False),
-    (GRAD, QKV, 0, 0), (MEAN, QKV, 0, 0, 0), (TOTAL, 0, True, True), (MEAN, UP, 0, 0, 1), (DONE, 0), (MEAN, QKV, 1, 0, 3),
-    (TOTAL, 1, True, False), (MEAN, OUT, 0, 0, 1), (MEAN, OUT, 1, 0, 4), (DONE, 1), (FINISH,), (MEAN, DOWN, 0, 0, 2), (MEAN, QKV, 1, 0, 4),
-    (MEAN, QKV, 0, 0, 1), (MEAN, DOWN, 0, 0, 3), (MEAN, UP, 0, 0, 2), (MEAN, OUT, 0, 0, 2), (MEAN, DOWN, 0, 0, 4), (MEAN, QKV, 0, 0, 2),
-    (MEAN, UP, 0, 0, 3), (MEAN, OUT, 0, 0, 3), (MEAN, QKV, 0, 0, 3), (MEAN, UP, 0, 0, 4), (MEAN, OUT, 0, 0, 4), (MEAN, QKV, 0, 0, 4),
-    (MEAN, DOWN, 1, 0, 5), (MEAN, UP, 1, 0, 5), (MEAN, OUT, 1, 0, 5), (MEAN, QKV, 1, 0, 5), (MEAN, DOWN, 0, 0, 5), (MEAN, OUT, 0, 0, 5),
-    (MEAN, UP, 0, 0, 5), (MEAN, QKV, 0, 0, 5),
+    (START,), (ACT, 1, 0), (ACT, 1, 1), (GRAD, DOWN, 1, 0), (FREE,), (MEAN, DOWN, 1, 0, 0), (WAIT_MLP, 1), (MLP, 1, 0, False), (SEND, 0),
+    (MLP, 1, 0, True), (PAIR, 0, True), (MLP, 1, 1, False), (SEND, 1), (MLP, 1, 1, True), (LOAD_MLP, 0), (PAIR, 1, True),
+    (MEAN, DOWN, 1, 0, 1), (GRAD, UP, 1, 0), (MEAN, UP, 1, 0, 0), (TOTAL, 0, False, True), (WAIT_ATTN, 1), (PROJECT, 1, 0), (PROJECT, 1, 1),
+    (DONE, 0), (LOAD_HEAD, 0, 0), (HEAD, 1, 0, 0), (MEAN, DOWN, 1, 0, 2), (HEAD, 1, 0, 1), (TOTAL, 1, False, False), (HEAD, 1, 0, 2),
+    (DONE, 1), (PART, 1, 0, False), (SEND, 0), (PART, 1, 0, True), (MEAN, UP, 1, 0, 1), (PAIR, 0, False), (LOAD_HEAD, 1, 0), (HEAD, 1, 1, 0),
+    (MEAN, DOWN, 1, 0, 3), (HEAD, 1, 1, 1), (HEAD, 1, 1, 2), (PART, 1, 1, False), (SEND, 1), (PART, 1, 1, True), (LOAD_ATTN, 0),
+    (GRAD, QKV, 1, 0), (MEAN, QKV, 1, 0, 0), (PAIR, 1, False), (MEAN, UP, 1, 0, 2), (MEAN, DOWN, 1, 0, 4), (GRAD, OUT, 1, 0), (FREE,),
+    (MEAN, OUT, 1, 0, 0), (TOTAL, 0, False, True), (WAIT_ATTN, 0), (PROJECT, 0, 0), (PROJECT, 0, 1), (DONE, 0), (WAIT_MLP, 0),
+    (MLP, 0, 0, False), (SEND, 0), (MLP, 0, 0, True), (TOTAL, 1, False, False), (PAIR, 0, False), (MEAN, QKV, 1, 0, 1), (MEAN, UP, 1, 0, 3),
+    (DONE, 1), (MLP, 0, 1, False), (SEND, 1), (MLP, 0, 1, True), (GRAD, DOWN, 0, 0), (MEAN, DOWN, 0, 0, 0), (GRAD, DOWN, 0, 1),
+    (MEAN, DOWN, 0, 1, 0), (GRAD, DOWN, 0, 2), (FREE,), (MEAN, DOWN, 0, 2, 0), (PAIR, 1, False), (TOTAL, 0, False, True), (MEAN, OUT, 1, 0, 1),
+    (MEAN, QKV, 1, 0, 2), (MEAN, UP, 1, 0, 4), (DONE, 0), (MEAN, DOWN, 0, 0, 1), (GRAD, UP, 0, 0), (MEAN, UP, 0, 0, 0), (MEAN, DOWN, 0, 1, 1),
+    (GRAD, UP, 0, 1), (MEAN, UP, 0, 1, 0), (MEAN, DOWN, 0, 2, 1), (LOAD_HEAD, 0, 0), (HEAD, 0, 0, 0), (TOTAL, 1, False, False),
+    (HEAD, 0, 0, 1), (DONE, 1), (MEAN, QKV, 1, 0, 3), (MEAN, OUT, 1, 0, 2), (HEAD, 0, 0, 2), (PART, 0, 0, False), (SEND, 0),
+    (PART, 0, 0, True), (MEAN, DOWN, 0, 0, 2), (PAIR, 0, False), (MEAN, DOWN, 0, 1, 2), (MEAN, QKV, 1, 0, 4), (MEAN, UP, 0, 0, 1),
+    (MEAN, DOWN, 0, 2, 2), (LOAD_HEAD, 1, 0), (HEAD, 0, 1, 0), (MEAN, OUT, 1, 0, 3), (HEAD, 0, 1, 1), (MEAN, UP, 0, 1, 1), (HEAD, 0, 1, 2),
+    (PART, 0, 1, False), (SEND, 1), (PART, 0, 1, True), (GRAD, QKV, 0, 0), (MEAN, QKV, 0, 0, 0), (PAIR, 1, False), (GRAD, QKV, 0, 1),
+    (MEAN, QKV, 0, 1, 0), (MEAN, OUT, 1, 0, 4), (MEAN, UP, 0, 0, 2), (MEAN, DOWN, 0, 0, 3), (MEAN, UP, 0, 1, 2), (MEAN, DOWN, 0, 1, 3),
+    (GRAD, OUT, 0, 0), (FREE,), (MEAN, OUT, 0, 0, 0), (TOTAL, 0, True, True), (MEAN, DOWN, 0, 2, 3), (DONE, 0), (MEAN, UP, 0, 0, 3),
+    (TOTAL, 1, True, False), (MEAN, DOWN, 0, 0, 4), (MEAN, QKV, 0, 0, 1), (DONE, 1), (FINISH,), (MEAN, QKV, 0, 1, 1), (MEAN, UP, 0, 1, 3),
+    (MEAN, DOWN, 0, 1, 4), (MEAN, DOWN, 0, 2, 4), (MEAN, UP, 0, 0, 4), (MEAN, QKV, 0, 0, 2), (MEAN, OUT, 0, 0, 1), (MEAN, QKV, 0, 1, 2),
+    (MEAN, OUT, 0, 0, 2), (MEAN, UP, 0, 1, 4), (MEAN, OUT, 0, 0, 3), (MEAN, OUT, 0, 0, 4), (MEAN, QKV, 0, 0, 3), (MEAN, QKV, 0, 1, 3),
+    (MEAN, QKV, 0, 0, 4), (MEAN, QKV, 0, 1, 4), (MEAN, DOWN, 1, 0, 5), (MEAN, UP, 1, 0, 5), (MEAN, QKV, 1, 0, 5), (MEAN, OUT, 1, 0, 5),
+    (MEAN, DOWN, 0, 0, 5), (MEAN, UP, 0, 0, 5), (MEAN, DOWN, 0, 1, 5), (MEAN, DOWN, 0, 2, 5), (MEAN, UP, 0, 1, 5), (MEAN, OUT, 0, 0, 5),
+    (MEAN, QKV, 0, 0, 5), (MEAN, QKV, 0, 1, 5),
 )
 
 
@@ -679,10 +772,10 @@
     def device_backward(x_saved, y_saved, d_out, w_qkv, w_out, w_up, w_down):
         layers, width, _, heads, d = w_qkv.shape
         by_head = jnp.transpose(w_qkv, (0, 2, 3, 1, 4))
-        d_in, down, up, qkv, out = backward(x_saved, y_saved, d_out, by_head, w_out, w_up, w_down, replicas)
-        g_qkv = jnp.transpose(widen(qkv, 3 * heads).reshape(layers, 3, heads, width, d), (0, 3, 1, 2, 4))
-        g_out = widen(out).reshape(w_out.shape)
-        return d_in, g_qkv, g_out, widen(up), widen(down)
+        d_in, *fins = backward(x_saved, y_saved, d_out, by_head, w_out, w_up, w_down, replicas)
+        d_in, down, up, qkv, out = finish(d_in, fins, heads)
+        g_qkv = jnp.transpose(qkv.reshape(layers, 3, heads, width, d), (0, 3, 1, 2, 4))
+        return d_in, g_qkv, out.reshape(w_out.shape), up.reshape(w_up.shape), down.reshape(w_down.shape)
 
     return jax.shard_map(
         device_backward,

time: 756 us -> 665 us (0.88)
  Pallas kernels: 739 us -> 653 us
    pallas_call x1, Pallas kernels: 704 us -> 619 us  [backward(): pl.pallas_call(functools.partial(mega_kernel, dims, ORDER), in_specs=[ANY...]
    pallas_call x4 -> x1, Pallas kernels: 34.7 us -> 34 us  [finish(): pl.pallas_call(functools.partial(finish_kernel, jobs), in_specs=[ANY] * l...]
where the time goes in v2:
time: 665 us; the launch traced here: 654 us
  Pallas kernels  653 us (98%)
    pallas_call x1, Pallas kernels, backward(): pl.pallas_call(functools.partial(mega_kernel, dims, ORDER), in_specs=[ANY...  619 us
    pallas_call x1, Pallas kernels, finish(): pl.pallas_call(functools.partial(finish_kernel, jobs), in_specs=[ANY] * l...  34 us

profile of v2, /device:TPU:0, one launch (start us, length us, event | category | flops | bytes accessed | tf_op | source)
XLA Modules:
  0.0 653.7 jit_solution(2884436924937816306)
XLA Ops:
  0.6 618.6 %backward.1 = (bf16[2,1024,1536]{2,1,0:T(8,128)(2,1)}, bf16[2048,1536]{1,0:T(8,128)(2,1)}, bf16[2048,1152]{1,0:T(8,128)(2,1)}, bf16[2,1536,1536]{2,1,0:T(8,128)(...) custom-call(bf16[2,2,1024,1536]{3,2,1,0:T(8,128)(2,1)} %refs_0_.1, ...), custom_call_target="tpu_custom_call" | custom-call | tf_op jit(solution)/shard_map/backward/pallas_call | solution.py:644
  619.2 34.0 %finish.1 = (bf16[2,1024,1536]{2,1,0:T(8,128)(2,1)}, f32[2,1,1536,1536]{3,2,1,0:T(8,128)}, f32[2,1,1536,1536]{3,2,1,0:T(8,128)}, f32[2,9,1536,128]{3,2,1,0:T(8,128)}, f32[2,1,384,1536]{3,2,1,0:T(8,128)}) custom-call(bf16[2,1024,1536]{2,1,0:T(8,128)(2,1)} %get-tuple-element.15.refs_0_, bf16[2,1536,1536]{2,1,0:T(8,128)(2,1)} %get-tuple-element.16.refs_1_, ...), custom_call_target="tpu_custom_call" | custom-call | tf_op jit(solution)/shard_map/finish/pallas_call | solution.py:714

commit v3 on v2

--- a/solution.py
+++ b/solution.py
@@ -290,16 +290,17 @@
         combine = Combine(self.wide, self.narrow, self.combine_sem)
         for l in range(self.layers):
             for kind in KINDS:
-                parts, first = self.cuts[kind, l]
-                g16, g32, a = tensors.pop(0), tensors.pop(0), tensors.pop(0)
-                rows = g16.shape[0] // parts
-                b0, b = (tensors.pop(0), tensors.pop(0)) if rows > first else (None, None)
-                self.grads[kind, l] = g16, g32, rows
-                for p in range(parts):
-                    a_bufs = [a.at[p, j] for j in range(4)]
-                    b_bufs = [b0.at[p]] + [b.at[p, j] for j in range(4)] if rows > first else None
+                g16, g32 = tensors.pop(0), tensors.pop(0)
+                self.grads[kind, l], base = (g16, g32), 0
+                for p, (rows, first) in enumerate(CUTS[l][kind]):
+                    a = tensors.pop(0)
+                    a_bufs, b_bufs = [a.at[j] for j in range(4)], None
+                    if rows > first:
+                        b0, b = tensors.pop(0), tensors.pop(0)
+                        b_bufs = [b0] + [b.at[j] for j in range(4)]
                     sems = self.dp_send.at[i], self.dp_recv.at[i]
-                    self.means[kind, l, p] = Mean(self.at, combine, self.replicas, p * rows, rows, first, g16, g32, self.fins[kind].at[l], a_bufs, b_bufs, *sems)
+                    self.means[kind, l, p] = Mean(self.at, combine, self.replicas, base, rows, first, g16, g32, self.fins[kind].at[l], a_bufs, b_bufs, *sems)
+                    base += rows
                     i += 1
 
     def local(self, k, src, dst):
@@ -497,9 +498,11 @@
 
     def grad(self, kind, l, part):
         rhs = (self.res, self.dh_v, self.dqkv_v, self.res)[kind]
-        g16, g32, rows = self.grads[kind, l]
+        g16, g32 = self.grads[kind, l]
         cols = g32.shape[1]
-        lo, hi = part * rows, (part + 1) * rows
+        sizes = [rows for rows, _ in CUTS[l][kind]]
+        lo, rows = sum(sizes[:part]), sizes[part]
+        hi = lo + rows
         tile = next(t for t in (256, 384, 128) if rows % t == 0)
         chunk = min(512 if cols % 512 == 0 else 384, cols)
         two = self.mbs * self.s
@@ -596,17 +599,14 @@
     shapes = (f, w), (w, f), (w, 3 * hd), (hd, w)
     hbm = {"d_in": (mbs, s, w), "act": (rows, f), "qkv_hbm": (rows, 3 * hd)}
     fins = [(layers, *shape) for shape in shapes]
-    cuts, tensors = {}, []
+    tensors = []
     for l in range(layers):
-        for k in KINDS:
-            r, c = shapes[k]
-            parts, share = CUTS[l][k]
-            n = r // parts
-            first = round(n * share / 32) * 32
-            cuts[k, l] = parts, first
-            tensors += [((r, c), BF16), ((r, c), F32), ((parts, 4, first // 2, c), BF16)]
-            if n > first:
-                tensors += [((parts, n - first, c), BF16), ((parts, 4, (n - first) // 2, c), BF16)]
+        for (r, c), cuts in zip(shapes, CUTS[l], strict=True):
+            tensors += [((r, c), BF16), ((r, c), F32)]
+            for n, first in cuts:
+                tensors += [((4, first // 2, c), BF16)]
+                if n > first:
+                    tensors += [((n - first, c), BF16), ((4, (n - first) // 2, c), BF16)]
     vmem = {
         "wu_v": (w, f),
         "wd_v": (f, w),
@@ -624,7 +624,7 @@
         "do_v": (s, d),
         "narrow": (2, 3, min(BLOCK, w // 2), w),
     }
-    n = sum(parts for parts, _ in cuts.values())
+    n = sum(len(cuts) for layer in CUTS for cuts in layer)
     dma, regular = pltpu.SemaphoreType.DMA, pltpu.SemaphoreType.REGULAR
     sems = {
         "dp_send": dma((n, 12)),
@@ -639,7 +639,7 @@
     }
     ins = ("x_saved", "y_saved", "d_out", "w_qkv", "w_out", "w_up", "w_down")
     names = ((*ins, *hbm), (*vmem, *sems))
-    dims = dict(names=names, count=len(tensors), layers=layers, mbs=mbs, s=s, w=w, f=f, heads=heads, hd=hd, replicas=replicas, cuts=cuts)
+    dims = dict(names=names, count=len(tensors), layers=layers, mbs=mbs, s=s, w=w, f=f, heads=heads, hd=hd, replicas=replicas)
     outs = [(v, BF16) for v in (*hbm.values(), *fins)] + tensors
     outs = pl.pallas_call(
         functools.partial(mega_kernel, dims, ORDER),
@@ -710,7 +710,7 @@
         blk = next(b for b in (256, 192, 128) if r % b == 0)
         jobs += [(which, l, lo, blk, pieces[which]) for l in range(layers) for lo in range(0, r, blk)]
     out = lambda a, p: jax.ShapeDtypeStruct(a.shape if not p else (a.shape[0], p, a.shape[1], a.shape[2] // p), F32 if p else BF16)
-    depth, width = 4, max(a.shape[2] for a in ins)
+    depth, width = 6, max(a.shape[2] for a in ins)
     return pl.pallas_call(
         functools.partial(finish_kernel, jobs),
         in_specs=[ANY] * len(ins),
@@ -727,35 +727,37 @@
 
 
 CUTS = (
-    ((3, 0.5833), (2, 1.0), (2, 0.6667), (1, 1.0)),
-    ((1, 0.5), (1, 0.5), (1, 0.5), (1, 1.0)),
+    (((896, 288), (384, 384), (128, 96), (128, 128)), ((896, 896), (512, 512), (128, 64)), ((512, 512), (1024, 640)), ((384, 384),)),
+    (((1536, 864),), ((1536, 704),), ((1536, 288),), ((384, 384),)),
 )
 ORDER = (
     (START,), (ACT, 1, 0), (ACT, 1, 1), (GRAD, DOWN, 1, 0), (FREE,), (MEAN, DOWN, 1, 0, 0), (WAIT_MLP, 1), (MLP, 1, 0, False), (SEND, 0),
-    (MLP, 1, 0, True), (PAIR, 0, True), (MLP, 1, 1, False), (SEND, 1), (MLP, 1, 1, True), (LOAD_MLP, 0), (PAIR, 1, True),
-    (MEAN, DOWN, 1, 0, 1), (GRAD, UP, 1, 0), (MEAN, UP, 1, 0, 0), (TOTAL, 0, False, True), (WAIT_ATTN, 1), (PROJECT, 1, 0), (PROJECT, 1, 1),
-    (DONE, 0), (LOAD_HEAD, 0, 0), (HEAD, 1, 0, 0), (MEAN, DOWN, 1, 0, 2), (HEAD, 1, 0, 1), (TOTAL, 1, False, False), (HEAD, 1, 0, 2),
-    (DONE, 1), (PART, 1, 0, False), (SEND, 0), (PART, 1, 0, True), (MEAN, UP, 1, 0, 1), (PAIR, 0, False), (LOAD_HEAD, 1, 0), (HEAD, 1, 1, 0),
-    (MEAN, DOWN, 1, 0, 3), (HEAD, 1, 1, 1), (HEAD, 1, 1, 2), (PART, 1, 1, False), (SEND, 1), (PART, 1, 1, True), (LOAD_ATTN, 0),
-    (GRAD, QKV, 1, 0), (MEAN, QKV, 1, 0, 0), (PAIR, 1, False), (MEAN, UP, 1, 0, 2), (MEAN, DOWN, 1, 0, 4), (GRAD, OUT, 1, 0), (FREE,),
-    (MEAN, OUT, 1, 0, 0), (TOTAL, 0, False, True), (WAIT_ATTN, 0), (PROJECT, 0, 0), (PROJECT, 0, 1), (DONE, 0), (WAIT_MLP, 0),
-    (MLP, 0, 0, False), (SEND, 0), (MLP, 0, 0, True), (TOTAL, 1, False, False), (PAIR, 0, False), (MEAN, QKV, 1, 0, 1), (MEAN, UP, 1, 0, 3),
-    (DONE, 1), (MLP, 0, 1, False), (SEND, 1), (MLP, 0, 1, True), (GRAD, DOWN, 0, 0), (MEAN, DOWN, 0, 0, 0), (GRAD, DOWN, 0, 1),
-    (MEAN, DOWN, 0, 1, 0), (GRAD, DOWN, 0, 2), (FREE,), (MEAN, DOWN, 0, 2, 0), (PAIR, 1, False), (TOTAL, 0, False, True), (MEAN, OUT, 1, 0, 1),
-    (MEAN, QKV, 1, 0, 2), (MEAN, UP, 1, 0, 4), (DONE, 0), (MEAN, DOWN, 0, 0, 1), (GRAD, UP, 0, 0), (MEAN, UP, 0, 0, 0), (MEAN, DOWN, 0, 1, 1),
-    (GRAD, UP, 0, 1), (MEAN, UP, 0, 1, 0), (MEAN, DOWN, 0, 2, 1), (LOAD_HEAD, 0, 0), (HEAD, 0, 0, 0), (TOTAL, 1, False, False),
-    (HEAD, 0, 0, 1), (DONE, 1), (MEAN, QKV, 1, 0, 3), (MEAN, OUT, 1, 0, 2), (HEAD, 0, 0, 2), (PART, 0, 0, False), (SEND, 0),
-    (PART, 0, 0, True), (MEAN, DOWN, 0, 0, 2), (PAIR, 0, False), (MEAN, DOWN, 0, 1, 2), (MEAN, QKV, 1, 0, 4), (MEAN, UP, 0, 0, 1),
-    (MEAN, DOWN, 0, 2, 2), (LOAD_HEAD, 1, 0), (HEAD, 0, 1, 0), (MEAN, OUT, 1, 0, 3), (HEAD, 0, 1, 1), (MEAN, UP, 0, 1, 1), (HEAD, 0, 1, 2),
-    (PART, 0, 1, False), (SEND, 1), (PART, 0, 1, True), (GRAD, QKV, 0, 0), (MEAN, QKV, 0, 0, 0), (PAIR, 1, False), (GRAD, QKV, 0, 1),
-    (MEAN, QKV, 0, 1, 0), (MEAN, OUT, 1, 0, 4), (MEAN, UP, 0, 0, 2), (MEAN, DOWN, 0, 0, 3), (MEAN, UP, 0, 1, 2), (MEAN, DOWN, 0, 1, 3),
-    (GRAD, OUT, 0, 0), (FREE,), (MEAN, OUT, 0, 0, 0), (TOTAL, 0, True, True), (MEAN, DOWN, 0, 2, 3), (DONE, 0), (MEAN, UP, 0, 0, 3),
-    (TOTAL, 1, True, False), (MEAN, DOWN, 0, 0, 4), (MEAN, QKV, 0, 0, 1), (DONE, 1), (FINISH,), (MEAN, QKV, 0, 1, 1), (MEAN, UP, 0, 1, 3),
-    (MEAN, DOWN, 0, 1, 4), (MEAN, DOWN, 0, 2, 4), (MEAN, UP, 0, 0, 4), (MEAN, QKV, 0, 0, 2), (MEAN, OUT, 0, 0, 1), (MEAN, QKV, 0, 1, 2),
-    (MEAN, OUT, 0, 0, 2), (MEAN, UP, 0, 1, 4), (MEAN, OUT, 0, 0, 3), (MEAN, OUT, 0, 0, 4), (MEAN, QKV, 0, 0, 3), (MEAN, QKV, 0, 1, 3),
-    (MEAN, QKV, 0, 0, 4), (MEAN, QKV, 0, 1, 4), (MEAN, DOWN, 1, 0, 5), (MEAN, UP, 1, 0, 5), (MEAN, QKV, 1, 0, 5), (MEAN, OUT, 1, 0, 5),
-    (MEAN, DOWN, 0, 0, 5), (MEAN, UP, 0, 0, 5), (MEAN, DOWN, 0, 1, 5), (MEAN, DOWN, 0, 2, 5), (MEAN, UP, 0, 1, 5), (MEAN, OUT, 0, 0, 5),
-    (MEAN, QKV, 0, 0, 5), (MEAN, QKV, 0, 1, 5),
+    (MLP, 1, 0, True), (PAIR, 0, True), (MLP, 1, 1, False), (SEND, 1), (MEAN, DOWN, 1, 0, 1), (MLP, 1, 1, True), (LOAD_MLP, 0),
+    (PAIR, 1, True), (GRAD, UP, 1, 0), (MEAN, UP, 1, 0, 0), (TOTAL, 0, False, True), (WAIT_ATTN, 1), (PROJECT, 1, 0), (DONE, 0),
+    (PROJECT, 1, 1), (LOAD_HEAD, 0, 0), (HEAD, 1, 0, 0), (MEAN, DOWN, 1, 0, 2), (HEAD, 1, 0, 1), (TOTAL, 1, False, False), (HEAD, 1, 0, 2),
+    (MEAN, UP, 1, 0, 1), (DONE, 1), (PART, 1, 0, False), (SEND, 0), (PART, 1, 0, True), (LOAD_HEAD, 1, 0), (HEAD, 1, 1, 0),
+    (MEAN, DOWN, 1, 0, 3), (PAIR, 0, False), (HEAD, 1, 1, 1), (HEAD, 1, 1, 2), (GRAD, QKV, 1, 0), (MEAN, QKV, 1, 0, 0), (MEAN, UP, 1, 0, 2),
+    (PART, 1, 1, False), (SEND, 1), (MEAN, DOWN, 1, 0, 4), (PART, 1, 1, True), (LOAD_ATTN, 0), (GRAD, OUT, 1, 0), (FREE,),
+    (MEAN, OUT, 1, 0, 0), (TOTAL, 0, False, True), (PAIR, 1, False), (WAIT_ATTN, 0), (PROJECT, 0, 0), (DONE, 0), (PROJECT, 0, 1),
+    (MEAN, QKV, 1, 0, 1), (WAIT_MLP, 0), (MLP, 0, 0, False), (SEND, 0), (MEAN, UP, 1, 0, 3), (MLP, 0, 0, True), (MEAN, OUT, 1, 0, 1),
+    (PAIR, 0, False), (TOTAL, 1, False, False), (MEAN, QKV, 1, 0, 2), (DONE, 1), (MLP, 0, 1, False), (SEND, 1), (MEAN, OUT, 1, 0, 2),
+    (MLP, 0, 1, True), (PAIR, 1, False), (MEAN, UP, 1, 0, 4), (GRAD, DOWN, 0, 0), (MEAN, DOWN, 0, 0, 0), (GRAD, DOWN, 0, 1),
+    (MEAN, DOWN, 0, 1, 0), (MEAN, QKV, 1, 0, 3), (GRAD, DOWN, 0, 2), (MEAN, DOWN, 0, 2, 0), (GRAD, DOWN, 0, 3), (FREE,), (MEAN, DOWN, 0, 3, 0),
+    (TOTAL, 0, False, True), (MEAN, OUT, 1, 0, 3), (GRAD, UP, 0, 0), (MEAN, UP, 0, 0, 0), (DONE, 0), (GRAD, UP, 0, 1), (MEAN, UP, 0, 1, 0),
+    (MEAN, DOWN, 0, 0, 1), (TOTAL, 1, False, False), (GRAD, UP, 0, 2), (MEAN, UP, 0, 2, 0), (LOAD_HEAD, 0, 0), (HEAD, 0, 0, 0),
+    (MEAN, QKV, 1, 0, 4), (MEAN, DOWN, 0, 1, 1), (MEAN, DOWN, 0, 2, 1), (MEAN, DOWN, 0, 3, 1), (DONE, 1), (HEAD, 0, 0, 1), (HEAD, 0, 0, 2),
+    (MEAN, DOWN, 0, 0, 2), (PART, 0, 0, False), (SEND, 0), (MEAN, DOWN, 0, 1, 2), (MEAN, DOWN, 0, 2, 2), (MEAN, OUT, 1, 0, 4),
+    (MEAN, DOWN, 0, 3, 2), (PART, 0, 0, True), (PAIR, 0, False), (MEAN, UP, 0, 0, 1), (LOAD_HEAD, 1, 0), (HEAD, 0, 1, 0),
+    (MEAN, DOWN, 0, 1, 3), (HEAD, 0, 1, 1), (MEAN, UP, 0, 1, 1), (MEAN, UP, 0, 2, 1), (MEAN, DOWN, 0, 3, 3), (HEAD, 0, 1, 2),
+    (GRAD, QKV, 0, 0), (MEAN, QKV, 0, 0, 0), (MEAN, UP, 0, 0, 2), (MEAN, DOWN, 0, 1, 4), (MEAN, DOWN, 0, 0, 3), (MEAN, DOWN, 0, 3, 4),
+    (MEAN, DOWN, 0, 2, 3), (GRAD, QKV, 0, 1), (MEAN, QKV, 0, 1, 0), (MEAN, UP, 0, 1, 2), (MEAN, UP, 0, 2, 2), (PART, 0, 1, False), (SEND, 1),
+    (PART, 0, 1, True), (GRAD, OUT, 0, 0), (FREE,), (MEAN, OUT, 0, 0, 0), (MEAN, QKV, 0, 0, 1), (MEAN, UP, 0, 0, 3), (TOTAL, 0, True, True),
+    (PAIR, 1, False), (DONE, 0), (MEAN, QKV, 0, 0, 2), (MEAN, DOWN, 0, 0, 4), (MEAN, DOWN, 0, 2, 4), (MEAN, QKV, 0, 1, 1), (MEAN, UP, 0, 0, 4),
+    (MEAN, UP, 0, 1, 3), (MEAN, OUT, 0, 0, 1), (MEAN, UP, 0, 2, 3), (TOTAL, 1, True, False), (MEAN, QKV, 0, 0, 3), (MEAN, OUT, 0, 0, 2),
+    (DONE, 1), (FINISH,), (MEAN, QKV, 0, 1, 2), (MEAN, UP, 0, 1, 4), (MEAN, UP, 0, 2, 4), (MEAN, OUT, 0, 0, 3), (MEAN, QKV, 0, 0, 4),
+    (MEAN, OUT, 0, 0, 4), (MEAN, QKV, 0, 1, 3), (MEAN, QKV, 0, 1, 4), (MEAN, DOWN, 1, 0, 5), (MEAN, UP, 1, 0, 5), (MEAN, QKV, 1, 0, 5),
+    (MEAN, OUT, 1, 0, 5), (MEAN, DOWN, 0, 1, 5), (MEAN, DOWN, 0, 3, 5), (MEAN, DOWN, 0, 0, 5), (MEAN, DOWN, 0, 2, 5), (MEAN, UP, 0, 0, 5),
+    (MEAN, UP, 0, 1, 5), (MEAN, UP, 0, 2, 5), (MEAN, QKV, 0, 0, 5), (MEAN, OUT, 0, 0, 5), (MEAN, QKV, 0, 1, 5),
 )
 
 

time: 665 us -> 654 us (0.983)
  Pallas kernels: 653 us -> 642 us
    pallas_call x1, Pallas kernels: 619 us -> 609 us  [backward(): pl.pallas_call(functools.partial(mega_kernel, dims, ORDER), in_specs=[ANY...]
where the time goes in v3:
time: 654 us; the launch traced here: 643 us
  Pallas kernels  642 us (98%)
    pallas_call x1, Pallas kernels, backward(): pl.pallas_call(functools.partial(mega_kernel, dims, ORDER), in_specs=[ANY...  609 us
    pallas_call x1, Pallas kernels, finish(): pl.pallas_call(functools.partial(finish_kernel, jobs), in_specs=[ANY] * l...  33.1 us

profile of v3, /device:TPU:0, one launch (start us, length us, event | category | flops | bytes accessed | tf_op | source)
XLA Modules:
  0.0 642.8 jit_solution(8340506474327148216)
XLA Ops:
  0.6 608.5 %backward.1 = (bf16[2,1024,1536]{2,1,0:T(8,128)(2,1)}, bf16[2048,1536]{1,0:T(8,128)(2,1)}, bf16[2048,1152]{1,0:T(8,128)(2,1)}, bf16[2,1536,1536]{2,1,0:T(8,128)(...) custom-call(bf16[2,2,1024,1536]{3,2,1,0:T(8,128)(2,1)} %refs_0_.1, ...), custom_call_target="tpu_custom_call" | custom-call | tf_op jit(solution)/shard_map/backward/pallas_call | solution.py:644
  609.2 33.1 %finish.1 = (bf16[2,1024,1536]{2,1,0:T(8,128)(2,1)}, f32[2,1,1536,1536]{3,2,1,0:T(8,128)}, f32[2,1,1536,1536]{3,2,1,0:T(8,128)}, f32[2,9,1536,128]{3,2,1,0:T(8,128)}, f32[2,1,384,1536]{3,2,1,0:T(8,128)}) custom-call(bf16[2,1024,1536]{2,1,0:T(8,128)(2,1)} %get-tuple-element.15.refs_0_, bf16[2,1536,1536]{2,1,0:T(8,128)(2,1)} %get-tuple-element.16.refs_1_, ...), custom_call_target="tpu_custom_call" | custom-call | tf_op jit(solution)/shard_map/finish/pallas_call | solution.py:714

commit v4 on v3

--- a/solution.py
+++ b/solution.py
@@ -94,7 +94,8 @@
 
     def __call__(self, fn, ins, out):
         rows, cols = out.shape
-        pieces = [(lo, min(self.rows, rows - lo)) for lo in range(0, rows, self.rows)]
+        size = -(-rows // (-(-rows // self.rows) * 32)) * 32
+        pieces = [(lo, min(size, rows - lo)) for lo in range(0, rows, size)]
         loads, bufs, stores = [], [], []
         for k, (lo, n) in enumerate(pieces):
             slot = k % 2
@@ -727,37 +728,34 @@
 
 
 CUTS = (
-    (((896, 288), (384, 384), (128, 96), (128, 128)), ((896, 896), (512, 512), (128, 64)), ((512, 512), (1024, 640)), ((384, 384),)),
-    (((1536, 864),), ((1536, 704),), ((1536, 288),), ((384, 384),)),
+    (((1024, 384), (512, 224)), ((896, 896), (640, 640)), ((1024, 640), (512, 384)), ((384, 384),)),
+    (((1536, 800),), ((1536, 992),), ((1536, 416),), ((384, 384),)),
 )
 ORDER = (
-    (START,), (ACT, 1, 0), (ACT, 1, 1), (GRAD, DOWN, 1, 0), (FREE,), (MEAN, DOWN, 1, 0, 0), (WAIT_MLP, 1), (MLP, 1, 0, False), (SEND, 0),
-    (MLP, 1, 0, True), (PAIR, 0, True), (MLP, 1, 1, False), (SEND, 1), (MEAN, DOWN, 1, 0, 1), (MLP, 1, 1, True), (LOAD_MLP, 0),
-    (PAIR, 1, True), (GRAD, UP, 1, 0), (MEAN, UP, 1, 0, 0), (TOTAL, 0, False, True), (WAIT_ATTN, 1), (PROJECT, 1, 0), (DONE, 0),
-    (PROJECT, 1, 1), (LOAD_HEAD, 0, 0), (HEAD, 1, 0, 0), (MEAN, DOWN, 1, 0, 2), (HEAD, 1, 0, 1), (TOTAL, 1, False, False), (HEAD, 1, 0, 2),
-    (MEAN, UP, 1, 0, 1), (DONE, 1), (PART, 1, 0, False), (SEND, 0), (PART, 1, 0, True), (LOAD_HEAD, 1, 0), (HEAD, 1, 1, 0),
-    (MEAN, DOWN, 1, 0, 3), (PAIR, 0, False), (HEAD, 1, 1, 1), (HEAD, 1, 1, 2), (GRAD, QKV, 1, 0), (MEAN, QKV, 1, 0, 0), (MEAN, UP, 1, 0, 2),
-    (PART, 1, 1, False), (SEND, 1), (MEAN, DOWN, 1, 0, 4), (PART, 1, 1, True), (LOAD_ATTN, 0), (GRAD, OUT, 1, 0), (FREE,),
-    (MEAN, OUT, 1, 0, 0), (TOTAL, 0, False, True), (PAIR, 1, False), (WAIT_ATTN, 0), (PROJECT, 0, 0), (DONE, 0), (PROJECT, 0, 1),
-    (MEAN, QKV, 1, 0, 1), (WAIT_MLP, 0), (MLP, 0, 0, False), (SEND, 0), (MEAN, UP, 1, 0, 3), (MLP, 0, 0, True), (MEAN, OUT, 1, 0, 1),
-    (PAIR, 0, False), (TOTAL, 1, False, False), (MEAN, QKV, 1, 0, 2), (DONE, 1), (MLP, 0, 1, False), (SEND, 1), (MEAN, OUT, 1, 0, 2),
-    (MLP, 0, 1, True), (PAIR, 1, False), (MEAN, UP, 1, 0, 4), (GRAD, DOWN, 0, 0), (MEAN, DOWN, 0, 0, 0), (GRAD, DOWN, 0, 1),
-    (MEAN, DOWN, 0, 1, 0), (MEAN, QKV, 1, 0, 3), (GRAD, DOWN, 0, 2), (MEAN, DOWN, 0, 2, 0), (GRAD, DOWN, 0, 3), (FREE,), (MEAN, DOWN, 0, 3, 0),
-    (TOTAL, 0, False, True), (MEAN, OUT, 1, 0, 3), (GRAD, UP, 0, 0), (MEAN, UP, 0, 0, 0), (DONE, 0), (GRAD, UP, 0, 1), (MEAN, UP, 0, 1, 0),
-    (MEAN, DOWN, 0, 0, 1), (TOTAL, 1, False, False), (GRAD, UP, 0, 2), (MEAN, UP, 0, 2, 0), (LOAD_HEAD, 0, 0), (HEAD, 0, 0, 0),
-    (MEAN, QKV, 1, 0, 4), (MEAN, DOWN, 0, 1, 1), (MEAN, DOWN, 0, 2, 1), (MEAN, DOWN, 0, 3, 1), (DONE, 1), (HEAD, 0, 0, 1), (HEAD, 0, 0, 2),
-    (MEAN, DOWN, 0, 0, 2), (PART, 0, 0, False), (SEND, 0), (MEAN, DOWN, 0, 1, 2), (MEAN, DOWN, 0, 2, 2), (MEAN, OUT, 1, 0, 4),
-    (MEAN, DOWN, 0, 3, 2), (PART, 0, 0, True), (PAIR, 0, False), (MEAN, UP, 0, 0, 1), (LOAD_HEAD, 1, 0), (HEAD, 0, 1, 0),
-    (MEAN, DOWN, 0, 1, 3), (HEAD, 0, 1, 1), (MEAN, UP, 0, 1, 1), (MEAN, UP, 0, 2, 1), (MEAN, DOWN, 0, 3, 3), (HEAD, 0, 1, 2),
-    (GRAD, QKV, 0, 0), (MEAN, QKV, 0, 0, 0), (MEAN, UP, 0, 0, 2), (MEAN, DOWN, 0, 1, 4), (MEAN, DOWN, 0, 0, 3), (MEAN, DOWN, 0, 3, 4),
-    (MEAN, DOWN, 0, 2, 3), (GRAD, QKV, 0, 1), (MEAN, QKV, 0, 1, 0), (MEAN, UP, 0, 1, 2), (MEAN, UP, 0, 2, 2), (PART, 0, 1, False), (SEND, 1),
-    (PART, 0, 1, True), (GRAD, OUT, 0, 0), (FREE,), (MEAN, OUT, 0, 0, 0), (MEAN, QKV, 0, 0, 1), (MEAN, UP, 0, 0, 3), (TOTAL, 0, True, True),
-    (PAIR, 1, False), (DONE, 0), (MEAN, QKV, 0, 0, 2), (MEAN, DOWN, 0, 0, 4), (MEAN, DOWN, 0, 2, 4), (MEAN, QKV, 0, 1, 1), (MEAN, UP, 0, 0, 4),
-    (MEAN, UP, 0, 1, 3), (MEAN, OUT, 0, 0, 1), (MEAN, UP, 0, 2, 3), (TOTAL, 1, True, False), (MEAN, QKV, 0, 0, 3), (MEAN, OUT, 0, 0, 2),
-    (DONE, 1), (FINISH,), (MEAN, QKV, 0, 1, 2), (MEAN, UP, 0, 1, 4), (MEAN, UP, 0, 2, 4), (MEAN, OUT, 0, 0, 3), (MEAN, QKV, 0, 0, 4),
-    (MEAN, OUT, 0, 0, 4), (MEAN, QKV, 0, 1, 3), (MEAN, QKV, 0, 1, 4), (MEAN, DOWN, 1, 0, 5), (MEAN, UP, 1, 0, 5), (MEAN, QKV, 1, 0, 5),
-    (MEAN, OUT, 1, 0, 5), (MEAN, DOWN, 0, 1, 5), (MEAN, DOWN, 0, 3, 5), (MEAN, DOWN, 0, 0, 5), (MEAN, DOWN, 0, 2, 5), (MEAN, UP, 0, 0, 5),
-    (MEAN, UP, 0, 1, 5), (MEAN, UP, 0, 2, 5), (MEAN, QKV, 0, 0, 5), (MEAN, OUT, 0, 0, 5), (MEAN, QKV, 0, 1, 5),
+    (START,), (ACT, 1, 1), (ACT, 1, 0), (GRAD, DOWN, 1, 0), (FREE,), (MEAN, DOWN, 1, 0, 0), (WAIT_MLP, 1), (MLP, 1, 0, False), (SEND, 0),
+    (MLP, 1, 0, True), (PAIR, 0, True), (MLP, 1, 1, False), (SEND, 1), (MLP, 1, 1, True), (MEAN, DOWN, 1, 0, 1), (GRAD, UP, 1, 0),
+    (MEAN, UP, 1, 0, 0), (WAIT_ATTN, 1), (PROJECT, 1, 0), (TOTAL, 0, False, True), (PAIR, 1, True), (PROJECT, 1, 1), (DONE, 0),
+    (LOAD_HEAD, 0, 0), (HEAD, 1, 0, 0), (MEAN, DOWN, 1, 0, 2), (HEAD, 1, 0, 1), (HEAD, 1, 0, 2), (PART, 1, 0, False), (SEND, 0),
+    (TOTAL, 1, False, False), (MEAN, UP, 1, 0, 1), (PART, 1, 0, True), (PAIR, 0, False), (MEAN, DOWN, 1, 0, 3), (DONE, 1), (LOAD_HEAD, 1, 0),
+    (HEAD, 1, 1, 0), (HEAD, 1, 1, 1), (HEAD, 1, 1, 2), (MEAN, UP, 1, 0, 2), (GRAD, OUT, 1, 0), (FREE,), (GRAD, QKV, 1, 0),
+    (MEAN, QKV, 1, 0, 0), (PART, 1, 1, False), (SEND, 1), (TOTAL, 0, False, True), (MEAN, DOWN, 1, 0, 4), (PART, 1, 1, True), (LOAD_ATTN, 0),
+    (PAIR, 1, False), (MEAN, OUT, 1, 0, 0), (LOAD_MLP, 0), (DONE, 0), (WAIT_MLP, 0), (MLP, 0, 0, False), (SEND, 0), (MEAN, QKV, 1, 0, 1),
+    (MEAN, UP, 1, 0, 3), (MLP, 0, 0, True), (WAIT_ATTN, 0), (PROJECT, 0, 0), (TOTAL, 1, False, False), (PAIR, 0, False), (MEAN, QKV, 1, 0, 2),
+    (MEAN, OUT, 1, 0, 1), (DONE, 1), (MLP, 0, 1, False), (SEND, 1), (MLP, 0, 1, True), (MEAN, UP, 1, 0, 4), (GRAD, DOWN, 0, 0),
+    (MEAN, DOWN, 0, 0, 0), (MEAN, QKV, 1, 0, 3), (GRAD, DOWN, 0, 1), (FREE,), (TOTAL, 0, False, True), (PAIR, 1, False), (GRAD, UP, 0, 0),
+    (MEAN, UP, 0, 0, 0), (MEAN, DOWN, 0, 0, 1), (MEAN, OUT, 1, 0, 2), (MEAN, DOWN, 0, 1, 0), (DONE, 0), (PROJECT, 0, 1), (GRAD, UP, 0, 1),
+    (MEAN, QKV, 1, 0, 4), (LOAD_HEAD, 0, 0), (HEAD, 0, 0, 0), (TOTAL, 1, False, False), (MEAN, DOWN, 0, 0, 2), (HEAD, 0, 0, 1),
+    (MEAN, UP, 0, 1, 0), (MEAN, DOWN, 0, 1, 1), (MEAN, OUT, 1, 0, 3), (MEAN, UP, 0, 0, 1), (HEAD, 0, 0, 2), (MEAN, DOWN, 0, 0, 3), (DONE, 1),
+    (LOAD_HEAD, 1, 0), (HEAD, 0, 1, 0), (MEAN, DOWN, 0, 1, 2), (HEAD, 0, 1, 1), (MEAN, UP, 0, 1, 1), (MEAN, UP, 0, 0, 2),
+    (MEAN, DOWN, 0, 0, 4), (PART, 0, 0, False), (SEND, 0), (HEAD, 0, 1, 2), (GRAD, OUT, 0, 0), (FREE,), (MEAN, OUT, 0, 0, 0),
+    (MEAN, DOWN, 0, 1, 3), (GRAD, QKV, 0, 0), (MEAN, UP, 0, 1, 2), (MEAN, OUT, 0, 0, 1), (MEAN, DOWN, 1, 0, 5), (MEAN, QKV, 0, 0, 0),
+    (MEAN, UP, 0, 0, 3), (MEAN, DOWN, 0, 1, 4), (MEAN, OUT, 1, 0, 4), (GRAD, QKV, 0, 1), (PART, 0, 0, True), (PAIR, 0, False),
+    (MEAN, DOWN, 0, 0, 5), (MEAN, QKV, 0, 1, 0), (PART, 0, 1, False), (SEND, 1), (MEAN, QKV, 0, 0, 1), (PART, 0, 1, True), (PAIR, 1, False),
+    (MEAN, OUT, 1, 0, 5), (MEAN, OUT, 0, 0, 2), (MEAN, UP, 0, 1, 3), (MEAN, UP, 0, 0, 4), (MEAN, QKV, 0, 0, 2), (MEAN, OUT, 0, 0, 3),
+    (MEAN, QKV, 0, 1, 1), (MEAN, UP, 0, 1, 4), (MEAN, QKV, 0, 1, 2), (MEAN, OUT, 0, 0, 4), (MEAN, QKV, 0, 0, 3), (MEAN, QKV, 0, 1, 3),
+    (TOTAL, 0, True, True), (MEAN, UP, 0, 1, 5), (MEAN, QKV, 0, 0, 4), (TOTAL, 1, True, False), (MEAN, QKV, 0, 1, 4), (DONE, 1),
+    (MEAN, OUT, 0, 0, 5), (DONE, 0), (MEAN, UP, 0, 0, 5), (MEAN, UP, 1, 0, 5), (FINISH,), (MEAN, QKV, 0, 0, 5), (MEAN, QKV, 1, 0, 5),
+    (MEAN, DOWN, 0, 1, 5), (MEAN, QKV, 0, 1, 5),
 )
 
 

time: 654 us -> 635 us (0.971)
  Pallas kernels: 642 us -> 622 us
    pallas_call x1, Pallas kernels: 609 us -> 589 us  [backward(): pl.pallas_call(functools.partial(mega_kernel, dims, ORDER), in_specs=[ANY...]
where the time goes in v4:
time: 635 us; the launch traced here: 623 us
  Pallas kernels  622 us (98%)
    pallas_call x1, Pallas kernels, backward(): pl.pallas_call(functools.partial(mega_kernel, dims, ORDER), in_specs=[ANY...  589 us
    pallas_call x1, Pallas kernels, finish(): pl.pallas_call(functools.partial(finish_kernel, jobs), in_specs=[ANY] * l...  33.1 us

profile of v4, /device:TPU:0, one launch (start us, length us, event | category | flops | bytes accessed | tf_op | source)
XLA Modules:
  0.0 623.3 jit_solution(2882149484622328485)
XLA Ops:
  0.6 589.3 %backward.1 = (bf16[2,1024,1536]{2,1,0:T(8,128)(2,1)}, bf16[2048,1536]{1,0:T(8,128)(2,1)}, bf16[2048,1152]{1,0:T(8,128)(2,1)}, bf16[2,1536,1536]{2,1,0:T(8,128)(...) custom-call(bf16[2,2,1024,1536]{3,2,1,0:T(8,128)(2,1)} %refs_0_.1, ...), custom_call_target="tpu_custom_call" | custom-call | tf_op jit(solution)/shard_map/backward/pallas_call | solution.py:645
  590.0 33.1 %finish.1 = (bf16[2,1024,1536]{2,1,0:T(8,128)(2,1)}, f32[2,1,1536,1536]{3,2,1,0:T(8,128)}, f32[2,1,1536,1536]{3,2,1,0:T(8,128)}, f32[2,9,1536,128]{3,2,1,0:T(8,128)}, f32[2,1,384,1536]{3,2,1,0:T(8,128)}) custom-call(bf16[2,1024,1536]{2,1,0:T(8,128)(2,1)} %get-tuple-element.15.refs_0_, bf16[2,1536,1536]{2,1,0:T(8,128)(2,1)} %get-tuple-element.16.refs_1_, ...), custom_call_target="tpu_custom_call" | custom-call | tf_op jit(solution)/shard_map/finish/pallas_call | solution.py:715

commit v5 on v4

--- a/solution.py
+++ b/solution.py
@@ -92,7 +92,7 @@
         self.wide, self.narrow, self.sem = wide, narrow, sem
         self.rows = wide.shape[1]
 
-    def __call__(self, fn, ins, out):
+    def __call__(self, fn, ins, out, ready, early=1):
         rows, cols = out.shape
         size = -(-rows // (-(-rows // self.rows) * 32)) * 32
         pieces = [(lo, min(size, rows - lo)) for lo in range(0, rows, size)]
@@ -106,7 +106,10 @@
             loads.append([pltpu.make_async_copy(part(r), b, self.sem.at[slot, q]) for q, (r, b) in enumerate(zip(ins, here))])
             bufs.append((here, mine))
             stores.append(pltpu.make_async_copy(mine, part(out), self.sem.at[slot, 3]))
-        for c in loads[0]:
+        for c in loads[0][:early]:
+            c.start()
+        ready()
+        for c in loads[0][early:]:
             c.start()
         for k, (lo, n) in enumerate(pieces):
             if k + 1 < len(pieces):
@@ -192,46 +195,46 @@
                     self.line(6).start()
 
         elif n == 1:
-            self.landed(0)
 
             @pl.when(at.outer)
             def _():
-                self.combine(lambda g, r: g + r, [self.a(self.g32, True), self.r0], self.s1)
+                self.combine(lambda g, r: g + r, [self.a(self.g32, True), self.r0], self.s1, lambda: self.landed(0))
                 self.line(1).start()
-
-            if two:
-
-                @pl.when(at.inner)
-                def _():
-                    self.landed(5)
-                    self.combine(lambda g, r: g + r, [self.b(self.g32, False, self.first), self.b(self.b0, False, 0)], self.t1)
-                    self.line(7).start()
-
-        elif n == 2:
 
             @pl.when(at.inner)
             def _():
-                self.landed(1)
-                self.combine(lambda g, r, q: g + r + q, [self.a(self.g32, True), self.r0, self.r1], self.s1)
+                self.landed(0)
+                if two:
+                    other = [self.b(self.g32, False, self.first), self.b(self.b0, False, 0)]
+                    self.combine(lambda g, r: g + r, other, self.t1, lambda: self.landed(5))
+                    self.line(7).start()
+
+        elif n == 2:
+
+            @pl.when(at.inner)
+            def _():
+                self.combine(lambda g, r, q: g + r + q, [self.a(self.g32, True), self.r0, self.r1], self.s1, lambda: self.landed(1), 2)
                 self.line(2).start()
                 if two:
-                    self.landed(6)
-                    self.landed(7)
+
+                    def folded():
+                        self.landed(6)
+                        self.landed(7)
+
                     own = [self.b(self.g32, True, self.first), self.b(self.b0, True, 0), self.b1]
-                    self.combine(lambda g, r, q: g + r + q, own, self.t2)
+                    self.combine(lambda g, r, q: g + r + q, own, self.t2, folded)
                     self.line(8).start()
 
         elif n == 3:
 
             @pl.when(at.inner)
             def _():
-                self.landed(2)
-                self.combine(lambda s, r: (s + r) * self.scale, [self.s1, self.r2], self.a(self.fin, True))
+                self.combine(lambda s, r: (s + r) * self.scale, [self.s1, self.r2], self.a(self.fin, True), lambda: self.landed(2))
                 self.line(3).start()
                 self.line(4).start()
                 if two:
-                    self.landed(8)
-                    self.combine(lambda s, r: (s + r) * self.scale, [self.t2, self.b2], self.b(self.fin, True, self.first))
+                    total = self.b(self.fin, True, self.first)
+                    self.combine(lambda s, r: (s + r) * self.scale, [self.t2, self.b2], total, lambda: self.landed(8))
                     self.line(9).start()
                     self.line(10).start()
 
@@ -711,7 +714,7 @@
         blk = next(b for b in (256, 192, 128) if r % b == 0)
         jobs += [(which, l, lo, blk, pieces[which]) for l in range(layers) for lo in range(0, r, blk)]
     out = lambda a, p: jax.ShapeDtypeStruct(a.shape if not p else (a.shape[0], p, a.shape[1], a.shape[2] // p), F32 if p else BF16)
-    depth, width = 6, max(a.shape[2] for a in ins)
+    depth, width = 8, max(a.shape[2] for a in ins)
     return pl.pallas_call(
         functools.partial(finish_kernel, jobs),
         in_specs=[ANY] * len(ins),

time: 635 us -> 634 us (level)
  no operation moved by 1% of the time
where the time goes in v5:
time: 634 us; the launch traced here: 623 us
  Pallas kernels  622 us (98%)
    pallas_call x1, Pallas kernels, backward(): pl.pallas_call(functools.partial(mega_kernel, dims, ORDER), in_specs=[ANY...  589 us
    pallas_call x1, Pallas kernels, finish(): pl.pallas_call(functools.partial(finish_kernel, jobs), in_specs=[ANY] * l...  33.1 us

profile of v5, /device:TPU:0, one launch (start us, length us, event | category | flops | bytes accessed | tf_op | source)
XLA Modules:
  0.0 622.6 jit_solution(4946072587422807261)
XLA Ops:
  0.6 588.6 %backward.1 = (bf16[2,1024,1536]{2,1,0:T(8,128)(2,1)}, bf16[2048,1536]{1,0:T(8,128)(2,1)}, bf16[2048,1152]{1,0:T(8,128)(2,1)}, bf16[2,1536,1536]{2,1,0:T(8,128)(...) custom-call(bf16[2,2,1024,1536]{3,2,1,0:T(8,128)(2,1)} %refs_0_.1, ...), custom_call_target="tpu_custom_call" | custom-call | tf_op jit(solution)/shard_map/backward/pallas_call | solution.py:648
  589.2 33.1 %finish.1 = (bf16[2,1024,1536]{2,1,0:T(8,128)(2,1)}, f32[2,1,1536,1536]{3,2,1,0:T(8,128)}, f32[2,1,1536,1536]{3,2,1,0:T(8,128)}, f32[2,9,1536,128]{3,2,1,0:T(8,128)}, f32[2,1,384,1536]{3,2,1,0:T(8,128)}) custom-call(bf16[2,1024,1536]{2,1,0:T(8,128)(2,1)} %get-tuple-element.15.refs_0_, bf16[2,1536,1536]{2,1,0:T(8,128)(2,1)} %get-tuple-element.16.refs_1_, ...), custom_call_target="tpu_custom_call" | custom-call | tf_op jit(solution)/shard_map/finish/pallas_call | solution.py:718
